TPU v7x, 32 devices: a whole 2x2x4 slice. The times are simulated.
32 devices in a mesh: dp: 2 (over core), expert: 16 (over z, y, x).
Axes of the slice: x: 2, y: 2, z: 4, core: 2. Of those that a mesh axis runs over, the one named last changes fastest.
Arguments:
- tokens: bfloat16 [8192, 1024], P(('dp', 'expert')), may hold values from -6 to 6
- ln_gain: float32 [1024], replicated, may hold values from 0.5 to 1.5
- router_weight: bfloat16 [1024, 16], replicated
- routes_expert: int32 [8192], P(('dp', 'expert')), may hold values from 0 to 15, as said below
- route_slot: int32 [8192], P(('dp', 'expert')), may hold values from -1 to 3, as said below
- w_in: bfloat16 [16, 1024, 4096], P('expert', None, 'dp'), may hold values from -0.1875 to 0.1875
- w_out: bfloat16 [16, 4096, 1024], P('expert', 'dp'), may hold values from -0.09375 to 0.09375
Outputs:
- mixed: bfloat16 [8192, 1024], P(('dp', 'expert'))
- expert_update: bfloat16 [8192, 1024], P(('dp', 'expert'))
Inputs may be any that keep to these rules, and one draw needn't show every extreme that they name: `routes_expert`: every expert is chosen by some token. route_slot[t] is the number of earlier tokens of the same device (the same aligned block of 256 tokens) routed to the same expert, or -1 where that number is 4 or more; the value 4 - 1 occurs in every draw.
All inputs are finite; a program needn't handle non-finite values.
Results may differ from a plain program's by a relative error of at most 0.0058.
Values may be sent and summed in bfloat16 or wider, within the bound.
No kernel may reach another device: no remote copies, remote signals or barrier semaphores. Data moves between devices by JAX's collectives and lax.ppermute only.
A program may use at most 64 MiB of HBM per device.

v0:
```python
import jax
import jax.numpy as jnp
from jax import lax
from jax.sharding import PartitionSpec as P

CAP = 4


def expert_rows(rows, weight_in, weight_out):
    hidden = jax.nn.gelu(
        jnp.einsum("sxcd,xdh->sxch", rows, weight_in, preferred_element_type=jnp.float32),
        approximate=True,
    ).astype(jnp.bfloat16)
    return jnp.einsum("sxch,xhd->sxcd", hidden, weight_out, preferred_element_type=jnp.float32)


def per_device(tokens, ln_gain, router_weight, routes_expert, route_slot, w_in, w_out):
    width = tokens.shape[1]
    values = tokens.astype(jnp.float32)
    mean = jnp.mean(values, axis=1, keepdims=True)
    var = jnp.mean((values - mean) ** 2, axis=1, keepdims=True)
    normed = ((values - mean) * lax.rsqrt(var + 1e-06) * ln_gain[None, :]).astype(jnp.bfloat16)
    logits = jnp.dot(normed, router_weight, preferred_element_type=jnp.float32)
    probs = jax.nn.softmax(logits, axis=1)
    expert_count = router_weight.shape[1]
    columns = jnp.arange(expert_count, dtype=jnp.int32)
    gate = jnp.sum(jnp.where(routes_expert[:, None] == columns[None, :], probs, 0.0), axis=1)
    kept = route_slot >= 0
    slot_rows = expert_count * CAP
    flat = jnp.where(kept, routes_expert * CAP + route_slot, slot_rows)
    outgoing = jnp.zeros((slot_rows, width), jnp.bfloat16).at[flat].set(normed, mode="drop")
    outgoing = outgoing.reshape(expert_count, CAP, width)
    local_experts = w_in.shape[0]
    block = lax.all_to_all(outgoing, "expert", split_axis=0, concat_axis=0, tiled=True)
    slots_here = block.shape[1]
    both_groups = lax.all_gather(block, "dp", axis=0, tiled=True)
    rows = both_groups.reshape(-1, local_experts, slots_here, width)
    partial_value = expert_rows(rows, w_in, w_out).reshape(-1, slots_here, width)
    summed = lax.psum_scatter(partial_value, "dp", scatter_dimension=0, tiled=True).astype(
        jnp.bfloat16
    )
    returned = lax.all_to_all(summed, "expert", split_axis=0, concat_axis=0, tiled=True)
    back = returned.reshape(slot_rows, width)[jnp.minimum(flat, slot_rows - 1)]
    update = jnp.where(kept[:, None], back, jnp.zeros_like(back))
    mixed = (values + gate[:, None] * update.astype(jnp.float32)).astype(jnp.bfloat16)
    return (mixed, update)


def solution(mesh):
    in_specs = (
        P(("dp", "expert"), None),
        P(),
        P(),
        P(("dp", "expert")),
        P(("dp", "expert")),
        P("expert", None, "dp"),
        P("expert", "dp", None),
    )
    out_specs = (P(("dp", "expert"), None), P(("dp", "expert"), None))
    return jax.shard_map(
        per_device, mesh=mesh, in_specs=in_specs, out_specs=out_specs, check_vma=False
    )
```

profile of v0, /device:TPU:0, one launch (start us, length us, event | category | flops | bytes accessed | tf_op | source)
XLA Modules:
  0.0 67.7 jit_solution(15074505845626651348)
XLA Ops:
  7.2 0.0 copy-start
  7.2 0.0 reduce-scatter.2.cloned.1.call-start
  7.2 1.2 %convert_reduce_fusion = f32[256]{0:T(256)S(1)} fusion(bf16[256,1024]{1,0:T(8,128)(2,1)} %param.7), kind=kLoop, calls=%fused_computation.10 | loop fusion | flops 524032 | bytes 525312 | tf_op jit(solution)/shard_map/reduce_sum | solution.py:20
  8.4 1.3 %fusion.9 = f32[256]{0:T(256)S(1)} fusion(bf16[256,1024]{1,0:T(8,128)(2,1)} %param.7, f32[256]{0:T(256)S(1)} %broadcast_multiply_fusion), kind=kLoop, calls=%fused_computation.13 | loop fusion | flops 1048320 | bytes 526336 | tf_op jit(solution)/shard_map/reduce_sum | solution.py:21
  9.8 0.7 %compare_select_fusion = (s32[256]{0:T(256)S(1)}, s32[256]{0:T(256)S(1)}) fusion(s32[256]{0:T(256)} %param.11, s32[256]{0:T(256)} %param.10), kind=kLoop, calls=%fused_computation.38 | loop fusion | flops 2816 | bytes 4096 | tf_op jit(solution)/shard_map/select_n | solution.py:43
  10.5 2.4 %scatter_custom_fusion = bf16[64,1024]{1,0:T(8,128)(2,1)S(1)} fusion(s32[256]{0:T(256)S(1)} %get-tuple-element.5, bf16[]{:T(256)} %constant.4.clone.1, bf16[256,1024]{1,0:T(8,128)(2,1)} %param.7, f32[1024]{0:T(1024)} %param.8, f32[256]{0:T(256)S(1)} %add_rsqrt_fusion, f32[256]{0:T(256)S(1)} %broadcast_multiply_fusion), kind=kCustom, calls=%fused_computation.31 | custom fusion | flops 1310720 | bytes 661506 | tf_op jit(solution)/shard_map/scatter | solution.py:31
  12.8 0.1 reshape.43
  12.9 15.9 %all_to_all.10 = bf16[16,4,1024]{2,1,0:T(4,128)(2,1)S(1)} all-to-all(bf16[16,4,1024]{2,1,0:T(4,128)(2,1)S(1)} %reshape.43), channel_id=1, replica_groups=mesh['dp'=2,'expert'=16] {'expert'}, dimensions={0} | all-to-all | bytes 262144 | tf_op jit(solution)/shard_map/all_to_all | solution.py:34
  28.9 2.0 %all_gather.3 = bf16[32,4,1024]{2,0,1:T(8,128)(2,1)S(1)} all-gather(bf16[16,4,1024]{2,0,1:T(8,128)(2,1)S(1)} %copy.11), channel_id=1, replica_groups=mesh['dp'=2,'expert'=16] {'dp'}, dimensions={0}, use_global_device_ids=true | all-gather | bytes 393216 | tf_op jit(solution)/shard_map/all_gather | solution.py:36
  30.9 0.0 copy-start.1
  30.9 0.0 copy-start.2
  30.9 0.0 copy-start.3
  30.9 0.0 copy-start.4
  30.9 5.9 %fusion = f32[32,4,1024]{2,0,1:T(8,128)} fusion(bf16[1,2048,1024]{2,1,0:T(8,128)(2,1)} %param.13, bf16[32,4,1024]{2,0,1:T(8,128)(2,1)S(1)} %all_gather.3, bf16[1,1024,2048]{2,1,0:T(8,128)(2,1)} %param.12), kind=kOutput, calls=%fused_computation.2 | convolution fusion | flops 1076101120 | bytes 9175040 | tf_op jit(solution)/shard_map/sxch,xhd->sxcd/dot_general | solution.py:14
  36.7 0.0 reduce-scatter.2.cloned.1.call-update
  36.8 0.0 copy-done
  36.8 0.0 copy-done.1
  36.8 0.0 copy-done.2
  36.8 0.4 fusion.41
  37.2 0.0 copy-done.3
  37.2 4.8 %reduce-scatter.2.cloned.1.call-done = f32[16,4,1024]{2,0,1:T(8,128)} async-done(((f32[32,4,1024]{2,0,1:T(8,128)}), f32[16,4,1024]{2,0,1:T(8,128)}) %reduce-scatter.2.cloned.1.call-update) | async-done | bytes 262160 | tf_op jit(solution)/shard_map/reduce_scatter | solution.py:39
  42.0 1.0 %convert_element_type.21 = bf16[16,4,1024]{2,0,1:T(8,128)(2,1)S(1)} convert(f32[16,4,1024]{2,0,1:T(8,128)} %reduce-scatter.2.cloned.1.call-done) | non-fusion elementwise | flops 65536 | bytes 393216 | tf_op jit(solution)/shard_map/convert_element_type | solution.py:39
  43.0 0.8 %copy.12 = bf16[16,4,1024]{2,1,0:T(4,128)(2,1)} copy(bf16[16,4,1024]{2,0,1:T(8,128)(2,1)S(1)} %convert_element_type.21) | data formatting | bytes 262144 | tf_op jit(solution)/shard_map/convert_element_type | solution.py:39
  43.8 6.7 %all-to-all-start.1 = ((bf16[16,4,1024]{2,1,0:T(4,128)(2,1)}), bf16[16,4,1024]{2,1,0:T(4,128)(2,1)S(1)}, u32[]{:S(2)}, u32[]{:S(2)}) async-start(bf16[16,4,1024]{2,1,0:T(4,128)(2,1)} %copy.12), calls=%async_computation.2 | async-start | bytes 262144 | tf_op jit(solution)/shard_map/all_to_all | solution.py:42
  50.5 0.0 copy-done.4
  50.5 7.9 %all-to-all-done.1 = bf16[16,4,1024]{2,1,0:T(4,128)(2,1)S(1)} async-done(((bf16[16,4,1024]{2,1,0:T(4,128)(2,1)}), bf16[16,4,1024]{2,1,0:T(4,128)(2,1)S(1)}, u32[]{:S(2)}, u32[]{:S(2)}) %all-to-all-start.1) | async-done | bytes 131104 | tf_op jit(solution)/shard_map/all_to_all | solution.py:42
  58.5 1.2 %gather_fusion = bf16[256,1024]{1,0:T(8,128)(2,1)S(1)} fusion(bf16[64,1024]{1,0:T(8,128)(2,1)S(1)} %reshape.47, s32[1024]{0:T(1024)S(1)} %pad_clamp_fusion), kind=kCustom, calls=%fused_computation | custom fusion | bytes 1049600 | tf_op jit(solution)/shard_map/gather | solution.py:43
  59.7 1.2 %fusion.12 = (bf16[256,1024]{1,0:T(8,128)(2,1)}, bf16[256,1024]{1,0:T(8,128)(2,1)}) fusion(bf16[256,1024]{1,0:T(8,128)(2,1)S(1)} %copy-done.1, f32[256]{0:T(256)S(1)} %select_reduce_fusion, bf16[256,1024]{1,0:T(8,128)(2,1)S(1)} %gather_fusion, pred[256]{0:T(512)(128)(4,1)S(1)} %broadcast_compare_fusion), kind=kLoop, calls=%fused_computation.16 | loop fusion | flops 1572864 | bytes 2098432 | tf_op jit(solution)/shard_map/convert_element_type | solution.py:45
  (8 shorter events, 0.2 us)
Async XLA Ops:
  7.2 29.6 %copy-start = (bf16[1024,16]{0,1:T(8,128)(2,1)S(1)}, bf16[1024,16]{0,1:T(8,128)(2,1)}, u32[]{:S(2)}) copy-start(bf16[1024,16]{0,1:T(8,128)(2,1)} %param.9) | copy-start | bytes 98308
  7.2 34.9 %reduce-scatter.2.cloned.1.call-start = ((), (), s32[]{:S(2)}) async-start(), calls=%async_computation.3 | async-start | bytes 786432 | tf_op jit(solution)/shard_map/reduce_scatter | solution.py:39
  30.9 5.9 %copy-start.1 = (bf16[256,1024]{1,0:T(8,128)(2,1)S(1)}, bf16[256,1024]{1,0:T(8,128)(2,1)}, u32[]{:S(2)}) copy-start(bf16[256,1024]{1,0:T(8,128)(2,1)} %param.7) | copy-start | bytes 1572868
  30.9 5.9 %copy-start.2 = (f32[1024]{0:T(1024)S(1)}, f32[1024]{0:T(1024)}, u32[]{:S(2)}) copy-start(f32[1024]{0:T(1024)} %param.8) | copy-start | bytes 12292
  30.9 6.3 %copy-start.3 = (s32[256]{0:T(256)S(1)}, s32[256]{0:T(256)}, u32[]{:S(2)}) copy-start(s32[256]{0:T(256)} %param.10) | copy-start | bytes 3076
  30.9 19.7 %copy-start.4 = (s32[256]{0:T(256)S(1)}, s32[256]{0:T(256)}, u32[]{:S(2)}) copy-start(s32[256]{0:T(256)} %param.11) | copy-start | bytes 3076
  43.8 14.7 %all-to-all-start.1 = ((bf16[16,4,1024]{2,1,0:T(4,128)(2,1)}), bf16[16,4,1024]{2,1,0:T(4,128)(2,1)S(1)}, u32[]{:S(2)}, u32[]{:S(2)}) async-start(bf16[16,4,1024]{2,1,0:T(4,128)(2,1)} %copy.12), calls=%async_computation.2 | async-start | bytes 262144 | tf_op jit(solution)/shard_map/all_to_all | solution.py:42
Sparse Core Ops, SparseCore 0:
  36.9 5.1 reduce-scatter.1
where the time goes:
time: 68.1 us; the launch traced here: 67.7 us
  blocking collectives  17.9 us (26%)
  between operations  14.1 us (21%)
  waiting for transfers between devices  12.8 us (19%)
  other arithmetic  7.81 us (11%)
  starting transfers between devices  6.77 us (10%)
  matrix products  6.22 us (9%)
  local copies, waits for them, and re-layouts  2.09 us (3%)
    all_to_all x1, blocking collectives, per_device(): lax.all_to_all(outgoing, 'expert', split_axis=0, concat_axis=0, tiled=True)  15.9 us
    all_to_all x1, waiting for transfers between devices, per_device(): lax.all_to_all(summed, 'expert', split_axis=0, concat_axis=0, tiled=True)  7.93 us
    all_to_all x1, starting transfers between devices, per_device(): lax.all_to_all(summed, 'expert', split_axis=0, concat_axis=0, tiled=True)  6.73 us
    dot_general x1, matrix products, expert_rows(): jnp.einsum('sxch,xhd->sxcd', hidden, weight_out, preferred_element_type=j...  5.86 us
    reduce_scatter x1, waiting for transfers between devices, per_device(): lax.psum_scatter(partial_value, 'dp', scatter_dimension=0, tiled=True)  4.82 us
    scatter x1, other arithmetic, per_device(): jnp.zeros((slot_rows, width), jnp.bfloat16).at[flat]  2.35 us
    all_gather x1, blocking collectives, per_device(): both_groups = lax.all_gather(block, 'dp', axis=0, tiled=True)  1.99 us
  transfers between devices with their start and end apart: 2, of which 2 were waited for; matrix products, arithmetic and copies ran while one was open for 1% of the time, Pallas kernels for 0%

commit v1 on v0

v1 whole, which is shorter than its diff:
```python
import functools

import jax
import jax.numpy as jnp
from jax import lax
from jax.experimental import pallas as pl
from jax.experimental.pallas import tpu as pltpu
from jax.sharding import PartitionSpec as P

CAP = 4
EPS = 1e-06
MIB = 1024 * 1024


def slot_of(expert_ref, slot_ref):
    expert = expert_ref[...]
    slot = slot_ref[...]
    return jnp.where(slot >= 0, expert * CAP + slot, -1)


def dispatch_body(tokens_ref, gain_ref, expert_ref, slot_ref, out_ref):
    slots, count = out_ref.shape[0], tokens_ref.shape[0]
    flat = slot_of(expert_ref, slot_ref)
    rows = lax.broadcasted_iota(jnp.int32, (slots, count), 0)
    select = jnp.where(rows == flat, 1.0, 0.0).astype(jnp.bfloat16)
    values = jnp.dot(select, tokens_ref[...], preferred_element_type=jnp.float32)
    mean = jnp.mean(values, axis=1, keepdims=True)
    centred = values - mean
    var = jnp.mean(centred * centred, axis=1, keepdims=True)
    normed = centred * lax.rsqrt(var + EPS) * gain_ref[...]
    out_ref[...] = normed.astype(jnp.bfloat16)


def gate_body(normed_ref, router_ref, expert_ref, slot_ref, pick_ref, gate_ref):
    count, slots = pick_ref.shape
    logits = lax.dot_general(
        router_ref[...],
        normed_ref[...],
        (((1,), (1,)), ((), ())),
        preferred_element_type=jnp.float32,
    )
    top = jnp.max(logits, axis=0, keepdims=True)
    exps = jnp.exp(logits - top)
    probs = exps / jnp.sum(exps, axis=0, keepdims=True)
    owner = lax.broadcasted_iota(jnp.int32, probs.shape, 1) // CAP
    expert = lax.broadcasted_iota(jnp.int32, probs.shape, 0)
    slot_gate = jnp.sum(jnp.where(owner == expert, probs, 0.0), axis=0, keepdims=True)
    flat = slot_of(expert_ref, slot_ref)
    column = jnp.transpose(jnp.broadcast_to(flat, (128, count)))[:, :1]
    picked = column == lax.broadcasted_iota(jnp.int32, (count, slots), 1)
    pick_ref[...] = jnp.where(picked, 1.0, 0.0).astype(jnp.bfloat16)
    gate = jnp.sum(jnp.where(picked, slot_gate, 0.0), axis=1, keepdims=True)
    gate_ref[...] = jnp.broadcast_to(gate, gate_ref.shape)


def gelu(v):
    inner = 0.7978845608028654 * (v + 0.044715 * (v * v * v))
    return 0.5 * v * (1.0 + jnp.tanh(inner))


def expert_body(own_ref, other_ref, w_in_ref, w_out_ref, keep_ref, send_ref, *, chunk):
    own = own_ref.shape[0]
    rows = jnp.concatenate([own_ref[...], other_ref[...]], axis=0)
    total = None
    for start in range(0, w_in_ref.shape[1], chunk):
        hidden = jnp.dot(
            rows, w_in_ref[:, start : start + chunk], preferred_element_type=jnp.float32
        )
        hidden = gelu(hidden).astype(jnp.bfloat16)
        part = jnp.dot(
            hidden, w_out_ref[start : start + chunk, :], preferred_element_type=jnp.float32
        )
        total = part if total is None else total + part
    keep_ref[...] = total[:own]
    send_ref[...] = total[own:]


def combine_body(tokens_ref, pick_ref, gate_ref, back_ref, mixed_ref, update_ref):
    update = jnp.dot(pick_ref[...], back_ref[...], preferred_element_type=jnp.float32)
    update_ref[...] = update.astype(jnp.bfloat16)
    mixed = tokens_ref[...].astype(jnp.float32) + gate_ref[:, :1] * update
    mixed_ref[...] = mixed.astype(jnp.bfloat16)


def params(limit):
    return pltpu.CompilerParams(vmem_limit_bytes=limit * MIB)


def per_device(tokens, ln_gain, router_weight, routes_expert, route_slot, w_in, w_out):
    count, width = tokens.shape
    experts = router_weight.shape[1]
    slots = experts * CAP
    swap = [(0, 1), (1, 0)]
    expert_row = routes_expert.reshape(1, count)
    slot_row = route_slot.reshape(1, count)
    outgoing = pl.pallas_call(
        dispatch_body,
        out_shape=jax.ShapeDtypeStruct((slots, width), jnp.bfloat16),
        compiler_params=params(8),
        name="dispatch",
    )(tokens, ln_gain.reshape(1, width), expert_row, slot_row)
    own = lax.all_to_all(
        outgoing.reshape(experts, CAP, width), "expert", split_axis=0, concat_axis=0, tiled=True
    ).reshape(slots, width)
    other = lax.ppermute(own, "dp", swap)
    pick, gate = pl.pallas_call(
        gate_body,
        out_shape=(
            jax.ShapeDtypeStruct((count, slots), jnp.bfloat16),
            jax.ShapeDtypeStruct((count, 128), jnp.float32),
        ),
        compiler_params=params(8),
        name="gate",
    )(outgoing, router_weight.T, expert_row, slot_row)
    keep, send = pl.pallas_call(
        functools.partial(expert_body, chunk=512),
        out_shape=(
            jax.ShapeDtypeStruct((slots, width), jnp.float32),
            jax.ShapeDtypeStruct((slots, width), jnp.float32),
        ),
        compiler_params=params(30),
        name="experts",
    )(own, other, w_in[0], w_out[0])
    summed = (keep + lax.ppermute(send, "dp", swap)).astype(jnp.bfloat16)
    back = lax.all_to_all(
        summed.reshape(experts, CAP, width), "expert", split_axis=0, concat_axis=0, tiled=True
    ).reshape(slots, width)
    block = count // 2
    mixed, update = pl.pallas_call(
        combine_body,
        grid=(count // block,),
        in_specs=[
            pl.BlockSpec((block, width), lambda i: (i, 0)),
            pl.BlockSpec((block, slots), lambda i: (i, 0)),
            pl.BlockSpec((block, 128), lambda i: (i, 0)),
            pl.BlockSpec((slots, width), lambda i: (0, 0)),
        ],
        out_specs=[
            pl.BlockSpec((block, width), lambda i: (i, 0)),
            pl.BlockSpec((block, width), lambda i: (i, 0)),
        ],
        out_shape=(
            jax.ShapeDtypeStruct((count, width), jnp.bfloat16),
            jax.ShapeDtypeStruct((count, width), jnp.bfloat16),
        ),
        compiler_params=params(12),
        name="combine",
    )(tokens, pick, gate, back)
    return (mixed, update)


def solution(mesh):
    in_specs = (
        P(("dp", "expert"), None),
        P(),
        P(),
        P(("dp", "expert")),
        P(("dp", "expert")),
        P("expert", None, "dp"),
        P("expert", "dp", None),
    )
    out_specs = (P(("dp", "expert"), None), P(("dp", "expert"), None))
    return jax.shard_map(
        per_device, mesh=mesh, in_specs=in_specs, out_specs=out_specs, check_vma=False
    )
```

time: 68.1 us -> 43.3 us (0.64)
  between operations: 14.1 us -> 0.73 us
  other arithmetic: 7.81 us -> 0.03 us
  local copies, waits for them, and re-layouts: 2.09 us -> 8.31 us
  matrix products: 6.22 us -> 0 us
  Pallas kernels: 0 us -> 3.64 us
  starting transfers between devices: 6.77 us -> 3.8 us
  waiting for transfers between devices: 12.8 us -> 10.4 us
  blocking collectives: 17.9 us -> 15.9 us
    unnamed x10 -> x20, local copies, waits for them, and re-layouts: 0.02 us -> 7.47 us
    dot_general x2 -> x0, matrix products: 6.22 us -> none  [the longest x1 5.86 us: expert_rows(): jnp.einsum('sxch,xhd->sxcd', hidden, weight_out, preferred_element_type=j...]
    reduce_scatter x1 -> x0, waiting for transfers between devices: 4.82 us -> none  [per_device(): lax.psum_scatter(partial_value, 'dp', scatter_dimension=0, tiled=True)]
    pallas_call x0 -> x4, Pallas kernels: none -> 3.64 us  [the longest x1 1.71 us: per_device(): pl.pallas_call(functools.partial(expert_body, chunk=512), out_shape=(jax....]
    all_to_all x1, starting transfers between devices: 6.73 us -> 3.51 us  [per_device(): lax.all_to_all(summed.reshape(experts, CAP, width), 'expert', split_axis=...]
    ppermute x0 -> x2, waiting for transfers between devices: none -> 2.72 us  [the longest x1 1.39 us: per_device(): summed = (keep + lax.ppermute(send, 'dp', swap)).astype(jnp.bfloat16)]
    reduce_sum x4 -> x0, other arithmetic: 2.57 us -> none  [the longest x1 1.32 us: per_device(): var = jnp.mean((values - mean) ** 2, axis=1, keepdims=True)]
    scatter x1 -> x0, other arithmetic: 2.35 us -> none  [per_device(): jnp.zeros((slot_rows, width), jnp.bfloat16).at[flat]]
  transfers between devices with their start and end apart: 2 -> 3, of which waited for: 2 -> 3; matrix products, arithmetic and copies ran while one was open for 1% -> 0% of each run, Pallas kernels for 0% -> 1%
where the time goes in v1:
time: 43.3 us; the launch traced here: 42.8 us
  blocking collectives  15.9 us (37%)
  waiting for transfers between devices  10.4 us (24%)
  local copies, waits for them, and re-layouts  8.31 us (19%)
  starting transfers between devices  3.8 us (9%)
  Pallas kernels  3.64 us (8%)
  between operations  0.73 us (2%)
    all_to_all x1, blocking collectives, per_device(): lax.all_to_all(outgoing.reshape(experts, CAP, width), 'expert', split_axi...  15.9 us
    all_to_all x1, waiting for transfers between devices, per_device(): lax.all_to_all(summed.reshape(experts, CAP, width), 'expert', split_axis=...  7.67 us
    unnamed x20, local copies, waits for them, and re-layouts  7.47 us
    all_to_all x1, starting transfers between devices, per_device(): lax.all_to_all(summed.reshape(experts, CAP, width), 'expert', split_axis=...  3.51 us
    pallas_call x1, Pallas kernels, per_device(): pl.pallas_call(functools.partial(expert_body, chunk=512), out_shape=(jax....  1.71 us
    ppermute x1, waiting for transfers between devices, per_device(): summed = (keep + lax.ppermute(send, 'dp', swap)).astype(jnp.bfloat16)  1.39 us
    ppermute x1, waiting for transfers between devices, per_device(): other = lax.ppermute(own, 'dp', swap)  1.33 us
    pallas_call x1, Pallas kernels, per_device(): pl.pallas_call(combine_body, grid=(count // block,), in_specs=[pl.BlockSp...  1.25 us
  transfers between devices with their start and end apart: 3, of which 3 were waited for; matrix products, arithmetic and copies ran while one was open for 0% of the time, Pallas kernels for 1%

profile of v1, /device:TPU:0, one launch (start us, length us, event | category | flops | bytes accessed | tf_op | source)
XLA Modules:
  0.0 42.8 jit_solution(4976148627658874102)
XLA Ops:
  0.6 0.0 copy-start.2
  0.6 1.0 %copy-done.2 = bf16[256,1024]{1,0:T(8,128)(2,1)S(1)} copy-done((bf16[256,1024]{1,0:T(8,128)(2,1)S(1)}, bf16[256,1024]{1,0:T(8,128)(2,1)}, u32[]{:S(2)}) %copy-start.2) | copy-done | bytes 524312
  1.7 0.0 copy-start.5
  1.7 0.7 %copy-done.5 = f32[1024]{0:T(1024)S(1)} copy-done((f32[1024]{0:T(1024)S(1)}, f32[1024]{0:T(1024)}, u32[]{:S(2)}) %copy-start.5) | copy-done | bytes 4120
  2.4 0.0 copy-start.6
  2.4 0.7 %copy-done.6 = s32[256]{0:T(256)S(1)} copy-done((s32[256]{0:T(256)S(1)}, s32[256]{0:T(256)}, u32[]{:S(2)}) %copy-start.6) | copy-done | bytes 1048
  3.0 0.0 copy-start.8
  3.0 0.7 %copy-done.8 = s32[256]{0:T(256)S(1)} copy-done((s32[256]{0:T(256)S(1)}, s32[256]{0:T(256)}, u32[]{:S(2)}) %copy-start.8) | copy-done | bytes 1048
  3.7 0.4 dispatch.1.normed_ref
  4.1 0.1 reshape.28
  4.2 15.9 %all_to_all.10 = bf16[16,4,1024]{2,1,0:T(4,128)(2,1)S(1)} all-to-all(bf16[16,4,1024]{2,1,0:T(4,128)(2,1)S(1)} %reshape.28), channel_id=1, replica_groups=mesh['dp'=2,'expert'=16] {'expert'}, dimensions={0} | all-to-all | bytes 262144 | tf_op jit(solution)/shard_map/all_to_all | solution.py:102
  20.2 0.1 collective-permute-start
  20.2 1.3 %collective-permute-done.other_ref = bf16[64,1024]{1,0:T(8,128)(2,1)S(1)} collective-permute-done((bf16[64,1024]{1,0:T(8,128)(2,1)S(1)}, bf16[64,1024]{1,0:T(8,128)(2,1)S(1)}, u32[]{:S(2)}, u32[]{:S(2)}) %collective-permute-start) | collective-permute-done | bytes 131104 | tf_op jit(solution)/shard_map/ppermute | solution.py:105
  21.6 0.0 copy-start
  21.6 2.2 %copy-done = bf16[1,1024,2048]{2,1,0:T(8,128)(2,1)S(1)} copy-done((bf16[1,1024,2048]{2,1,0:T(8,128)(2,1)S(1)}, bf16[1,1024,2048]{2,1,0:T(8,128)(2,1)}, u32[]{:S(2)}) %copy-start) | copy-done | bytes 4194328
  23.8 0.0 copy-start.1
  23.8 2.2 %copy-done.1 = bf16[1,2048,1024]{2,1,0:T(8,128)(2,1)S(1)} copy-done((bf16[1,2048,1024]{2,1,0:T(8,128)(2,1)S(1)}, bf16[1,2048,1024]{2,1,0:T(8,128)(2,1)}, u32[]{:S(2)}) %copy-start.1) | copy-done | bytes 4194328
  25.9 0.0 copy-start.4
  25.9 0.0 copy-start.7
  26.0 0.0 copy-start.9
  26.0 0.0 copy-start.3
  26.0 1.7 %experts.1 = (f32[64,1024]{1,0:T(8,128)S(1)}, f32[64,1024]{1,0:T(8,128)S(1)}) custom-call(bf16[64,1024]{1,0:T(8,128)(2,1)S(1)} %reshape.29.own_ref, bf16[64,1024]{1,0:T(8,128)(2,1)S(1)} %collective-permute-done.other_ref, bf16[1024,2048]{1,0:T(8,128)(2,1)S(1)} %bitcast.6, bf16[2048,1024]{1,0:T(8,128)(2,1)S(1)} %bitcast.7), custom_call_target="tpu_custom_call" | custom-call | tf_op jit(solution)/shard_map/experts/pallas_call | solution.py:115
  27.7 0.2 collective-permute-start.1
  27.9 1.4 %collective-permute-done.1 = f32[64,1024]{1,0:T(8,128)S(1)} collective-permute-done((f32[64,1024]{1,0:T(8,128)S(1)}, f32[64,1024]{1,0:T(8,128)S(1)}, u32[]{:S(2)}, u32[]{:S(2)}) %collective-permute-start.1) | collective-permute-done | bytes 262176 | tf_op jit(solution)/shard_map/ppermute | solution.py:124
  29.3 0.7 %reshape.30 = bf16[16,4,1024]{2,1,0:T(4,128)(2,1)} reshape(bf16[64,1024]{1,0:T(8,128)(2,1)S(1)} %add_convert_fusion) | data formatting | bytes 262144 | tf_op jit(solution)/shard_map/reshape | solution.py:126
  30.0 3.5 %all-to-all-start.1 = ((bf16[16,4,1024]{2,1,0:T(4,128)(2,1)}), bf16[16,4,1024]{2,1,0:T(4,128)(2,1)S(1)}, u32[]{:S(2)}, u32[]{:S(2)}) async-start(bf16[16,4,1024]{2,1,0:T(4,128)(2,1)} %reshape.30), calls=%async_computation.1 | async-start | bytes 262144 | tf_op jit(solution)/shard_map/all_to_all | solution.py:125
  33.5 0.0 copy-done.4
  33.6 0.0 copy-done.7
  33.6 0.0 copy-done.9
  33.6 0.3 gate.1
  33.9 7.7 %all-to-all-done.1 = bf16[16,4,1024]{2,1,0:T(4,128)(2,1)S(1)} async-done(((bf16[16,4,1024]{2,1,0:T(4,128)(2,1)}), bf16[16,4,1024]{2,1,0:T(4,128)(2,1)S(1)}, u32[]{:S(2)}, u32[]{:S(2)}) %all-to-all-start.1) | async-done | bytes 131104 | tf_op jit(solution)/shard_map/all_to_all | solution.py:125
  41.6 0.0 copy-done.3
  41.6 1.2 %combine.1 = (bf16[256,1024]{1,0:T(8,128)(2,1)}, bf16[256,1024]{1,0:T(8,128)(2,1)}) custom-call(bf16[256,1024]{1,0:T(8,128)(2,1)S(1)} %copy-done.3, bf16[256,64]{1,0:T(8,128)(2,1)S(1)} %get-tuple-element.6.pick_ref, f32[256,128]{1,0:T(8,128)S(1)} %get-tuple-element.7.gate_ref, bf16[64,1024]{1,0:T(8,128)(2,1)S(1)} %reshape.31.back_ref), custom_call_target="tpu_custom_call" | custom-call | tf_op jit(solution)/shard_map/combine/pallas_call | solution.py:129
  (3 shorter events, 0.1 us)
Async XLA Ops:
  0.6 1.0 %copy-start.2 = (bf16[256,1024]{1,0:T(8,128)(2,1)S(1)}, bf16[256,1024]{1,0:T(8,128)(2,1)}, u32[]{:S(2)}) copy-start(bf16[256,1024]{1,0:T(8,128)(2,1)} %tokens_ref.3) | copy-start | bytes 1572868
  1.7 0.7 %copy-start.5 = (f32[1024]{0:T(1024)S(1)}, f32[1024]{0:T(1024)}, u32[]{:S(2)}) copy-start(f32[1024]{0:T(1024)} %param.8) | copy-start | bytes 12292
  2.4 0.7 %copy-start.6 = (s32[256]{0:T(256)S(1)}, s32[256]{0:T(256)}, u32[]{:S(2)}) copy-start(s32[256]{0:T(256)} %param.10) | copy-start | bytes 3076
  3.0 0.7 %copy-start.8 = (s32[256]{0:T(256)S(1)}, s32[256]{0:T(256)}, u32[]{:S(2)}) copy-start(s32[256]{0:T(256)} %param.11) | copy-start | bytes 3076
  20.2 1.4 %collective-permute-start = (bf16[64,1024]{1,0:T(8,128)(2,1)S(1)}, bf16[64,1024]{1,0:T(8,128)(2,1)S(1)}, u32[]{:S(2)}, u32[]{:S(2)}) collective-permute-start(bf16[64,1024]{1,0:T(8,128)(2,1)S(1)} %reshape.29.own_ref), channel_id=1, source_target_pairs={{0,16},{16,0},{1,17},{17,1},{2,18},{18,2},{3,19},{19,3},{4,20},{20... | collective-permute-start | bytes 393224 | tf_op jit(solution)/shard_map/ppermute | solution.py:105
  21.6 2.2 %copy-start = (bf16[1,1024,2048]{2,1,0:T(8,128)(2,1)S(1)}, bf16[1,1024,2048]{2,1,0:T(8,128)(2,1)}, u32[]{:S(2)}) copy-start(bf16[1,1024,2048]{2,1,0:T(8,128)(2,1)} %param.12) | copy-start | bytes 12582916
  23.8 2.2 %copy-start.1 = (bf16[1,2048,1024]{2,1,0:T(8,128)(2,1)S(1)}, bf16[1,2048,1024]{2,1,0:T(8,128)(2,1)}, u32[]{:S(2)}) copy-start(bf16[1,2048,1024]{2,1,0:T(8,128)(2,1)} %param.13) | copy-start | bytes 12582916
  25.9 7.6 %copy-start.4 = (bf16[1024,16]{0,1:T(8,128)(2,1)S(1)}, bf16[1024,16]{0,1:T(8,128)(2,1)}, u32[]{:S(2)}) copy-start(bf16[1024,16]{0,1:T(8,128)(2,1)} %param.9) | copy-start | bytes 98308
  25.9 7.6 %copy-start.7 = (s32[256]{0:T(256)S(1)}, s32[256]{0:T(256)}, u32[]{:S(2)}) copy-start(s32[256]{0:T(256)} %param.10) | copy-start | bytes 3076
  26.0 7.6 %copy-start.9 = (s32[256]{0:T(256)S(1)}, s32[256]{0:T(256)}, u32[]{:S(2)}) copy-start(s32[256]{0:T(256)} %param.11) | copy-start | bytes 3076
  26.0 15.6 %copy-start.3 = (bf16[256,1024]{1,0:T(8,128)(2,1)S(1)}, bf16[256,1024]{1,0:T(8,128)(2,1)}, u32[]{:S(2)}) copy-start(bf16[256,1024]{1,0:T(8,128)(2,1)} %tokens_ref.3) | copy-start | bytes 1572868
  27.7 1.6 %collective-permute-start.1 = (f32[64,1024]{1,0:T(8,128)S(1)}, f32[64,1024]{1,0:T(8,128)S(1)}, u32[]{:S(2)}, u32[]{:S(2)}) collective-permute-start(f32[64,1024]{1,0:T(8,128)S(1)} %get-tuple-element.9), channel_id=1, source_target_pairs={{0,16},{16,0},{1,17},{17,1},{2,18},{18,2},{3,19},{19,3},{4,20},{20... | collective-permute-start | bytes 786440 | tf_op jit(solution)/shard_map/ppermute | solution.py:124
  30.0 11.5 %all-to-all-start.1 = ((bf16[16,4,1024]{2,1,0:T(4,128)(2,1)}), bf16[16,4,1024]{2,1,0:T(4,128)(2,1)S(1)}, u32[]{:S(2)}, u32[]{:S(2)}) async-start(bf16[16,4,1024]{2,1,0:T(4,128)(2,1)} %reshape.30), calls=%async_computation.1 | async-start | bytes 262144 | tf_op jit(solution)/shard_map/all_to_all | solution.py:125

commit v2 on v1

v2 whole, which is shorter than its diff:
```python
import functools

import jax
import jax.numpy as jnp
from jax import lax
from jax.experimental import pallas as pl
from jax.experimental.pallas import tpu as pltpu
from jax.sharding import PartitionSpec as P

CAP = 4
EPS = 1e-06
MIB = 1024 * 1024


def rotation(count):
    return (5 * count) // 8


def slot_of(expert, slot, experts):
    place = (expert + (experts - rotation(experts))) % experts
    return jnp.where(slot >= 0, place * CAP + slot, -1)


def open_body(out_ref):
    out_ref[...] = jnp.zeros(out_ref.shape, out_ref.dtype)


def select_body(opened_ref, tokens_ref, expert_ref, slot_ref, out_ref):
    del opened_ref
    slots, count = out_ref.shape[0], tokens_ref.shape[0]
    flat = slot_of(expert_ref[...], slot_ref[...], slots // CAP)
    rows = lax.broadcasted_iota(jnp.int32, (slots, count), 0)
    select = jnp.where(rows == flat, 1.0, 0.0).astype(jnp.bfloat16)
    out_ref[...] = jnp.dot(select, tokens_ref[...], preferred_element_type=jnp.float32)


def norm_body(values_ref, gain_ref, out_ref):
    values = values_ref[...]
    mean = jnp.mean(values, axis=1, keepdims=True)
    centred = values - mean
    var = jnp.mean(centred * centred, axis=1, keepdims=True)
    normed = centred * lax.rsqrt(var + EPS) * gain_ref[...]
    out_ref[...] = normed.reshape(out_ref.shape).astype(jnp.bfloat16)


def gate_body(normed_ref, router_ref, expert_ref, slot_ref, after_ref, pick_ref, gate_ref):
    del after_ref
    count, slots = pick_ref.shape
    experts = router_ref.shape[0]
    logits = lax.dot_general(
        router_ref[...],
        normed_ref[...].reshape(slots, normed_ref.shape[2]),
        (((1,), (1,)), ((), ())),
        preferred_element_type=jnp.float32,
    )
    top = jnp.max(logits, axis=0, keepdims=True)
    exps = jnp.exp(logits - top)
    probs = exps / jnp.sum(exps, axis=0, keepdims=True)
    place = lax.broadcasted_iota(jnp.int32, probs.shape, 1) // CAP
    owner = (place + rotation(experts)) % experts
    expert = lax.broadcasted_iota(jnp.int32, probs.shape, 0)
    slot_gate = jnp.sum(jnp.where(owner == expert, probs, 0.0), axis=0, keepdims=True)
    flat = slot_of(expert_ref[...], slot_ref[...], experts)
    column = jnp.transpose(jnp.broadcast_to(flat, (128, count)))[:, :1]
    picked = column == lax.broadcasted_iota(jnp.int32, (count, slots), 1)
    pick_ref[...] = jnp.where(picked, 1.0, 0.0).astype(jnp.bfloat16)
    gate = jnp.sum(jnp.where(picked, slot_gate, 0.0), axis=1, keepdims=True)
    gate_ref[...] = jnp.broadcast_to(gate, gate_ref.shape)


def gelu(v):
    inner = 0.7978845608028654 * (v + 0.044715 * (v * v * v))
    return 0.5 * v * (1.0 + jnp.tanh(inner))


def expert_body(rows_ref, w_in_ref, w_out_ref, out_ref, *, chunk):
    rows = rows_ref[...].reshape(out_ref.shape)
    total = None
    for start in range(0, w_in_ref.shape[1], chunk):
        hidden = jnp.dot(
            rows, w_in_ref[:, start : start + chunk], preferred_element_type=jnp.float32
        )
        hidden = gelu(hidden).astype(jnp.bfloat16)
        part = jnp.dot(
            hidden, w_out_ref[start : start + chunk, :], preferred_element_type=jnp.float32
        )
        total = part if total is None else total + part
    out_ref[...] = total


def join_body(keep_ref, other_ref, after_ref, out_ref):
    del after_ref
    total = keep_ref[...] + other_ref[...]
    out_ref[...] = total.reshape(out_ref.shape).astype(jnp.bfloat16)


def combine_body(tokens_ref, pick_ref, gate_ref, back_ref, mixed_ref, update_ref):
    back = back_ref[...].reshape(pick_ref.shape[1], back_ref.shape[2])
    update = jnp.dot(pick_ref[...], back, preferred_element_type=jnp.float32)
    update_ref[...] = update.astype(jnp.bfloat16)
    mixed = tokens_ref[...].astype(jnp.float32) + gate_ref[:, :1] * update
    mixed_ref[...] = mixed.astype(jnp.bfloat16)


def params(limit):
    return pltpu.CompilerParams(vmem_limit_bytes=limit * MIB)


def exchange(blocks):
    count = blocks.shape[0]
    group = [(i + rotation(count)) % count for i in range(count)]
    return lax.all_to_all(
        blocks, "expert", split_axis=0, concat_axis=0, tiled=True, axis_index_groups=[group]
    )


def per_device(tokens, ln_gain, router_weight, routes_expert, route_slot, w_in, w_out):
    count, width = tokens.shape
    experts = router_weight.shape[1]
    slots = experts * CAP
    swap = [(0, 1), (1, 0)]
    anywhere = pl.BlockSpec(memory_space=pl.ANY)
    whole = pl.BlockSpec(memory_space=pltpu.VMEM)
    expert_row = routes_expert.reshape(1, count)
    slot_row = route_slot.reshape(1, count)
    long = pl.CostEstimate(flops=20 * 10**9, bytes_accessed=32 * MIB, transcendentals=0)
    opened = pl.pallas_call(
        open_body,
        out_shape=jax.ShapeDtypeStruct((8, 128), jnp.float32),
        compiler_params=params(8),
        cost_estimate=long,
        name="open",
    )()
    values = pl.pallas_call(
        select_body,
        in_specs=[anywhere] + [whole] * 3,
        out_shape=jax.ShapeDtypeStruct((slots, width), jnp.float32),
        compiler_params=params(8),
        name="select",
    )(opened, tokens, expert_row, slot_row)
    outgoing = pl.pallas_call(
        norm_body,
        out_shape=jax.ShapeDtypeStruct((experts, CAP, width), jnp.bfloat16),
        compiler_params=params(8),
        cost_estimate=long,
        name="norm",
    )(values, ln_gain.reshape(1, width))
    own = exchange(outgoing)
    other = lax.ppermute(own, "dp", swap)
    serve = pl.pallas_call(
        functools.partial(expert_body, chunk=512),
        out_shape=jax.ShapeDtypeStruct((slots, width), jnp.float32),
        compiler_params=params(24),
        name="experts",
    )
    keep = serve(own, w_in[0], w_out[0])
    send = serve(other, w_in[0], w_out[0])
    pick, gate = pl.pallas_call(
        gate_body,
        in_specs=[whole] * 4 + [anywhere],
        out_shape=(
            jax.ShapeDtypeStruct((count, slots), jnp.bfloat16),
            jax.ShapeDtypeStruct((count, 128), jnp.float32),
        ),
        compiler_params=params(8),
        name="gate",
    )(outgoing, router_weight.T, expert_row, slot_row, send)
    summed = pl.pallas_call(
        join_body,
        in_specs=[whole] * 2 + [anywhere],
        out_shape=jax.ShapeDtypeStruct((experts, CAP, width), jnp.bfloat16),
        compiler_params=params(8),
        name="join",
    )(keep, lax.ppermute(send, "dp", swap), gate)
    back = exchange(summed)
    block = count // 2
    mixed, update = pl.pallas_call(
        combine_body,
        grid=(count // block,),
        in_specs=[
            pl.BlockSpec((block, width), lambda i: (i, 0)),
            pl.BlockSpec((block, slots), lambda i: (i, 0)),
            pl.BlockSpec((block, 128), lambda i: (i, 0)),
            pl.BlockSpec((experts, CAP, width), lambda i: (0, 0, 0)),
        ],
        out_specs=[
            pl.BlockSpec((block, width), lambda i: (i, 0)),
            pl.BlockSpec((block, width), lambda i: (i, 0)),
        ],
        out_shape=(
            jax.ShapeDtypeStruct((count, width), jnp.bfloat16),
            jax.ShapeDtypeStruct((count, width), jnp.bfloat16),
        ),
        compiler_params=params(12),
        name="combine",
    )(tokens, pick, gate, back)
    return (mixed, update)


def solution(mesh):
    in_specs = (
        P(("dp", "expert"), None),
        P(),
        P(),
        P(("dp", "expert")),
        P(("dp", "expert")),
        P("expert", None, "dp"),
        P("expert", "dp", None),
    )
    out_specs = (P(("dp", "expert"), None), P(("dp", "expert"), None))
    return jax.shard_map(
        per_device, mesh=mesh, in_specs=in_specs, out_specs=out_specs, check_vma=False
    )
```

time: 43.3 us -> 33.2 us (0.77)
  waiting for transfers between devices: 10.4 us -> 1.35 us
  blocking collectives: 15.9 us -> 23.8 us
  local copies, waits for them, and re-layouts: 8.31 us -> 1.03 us
  starting transfers between devices: 3.8 us -> 0.22 us
  Pallas kernels: 3.64 us -> 5.78 us
    all_to_all x1 -> x2, blocking collectives: 15.9 us -> 23.8 us  [exchange(): lax.all_to_all(blocks, 'expert', split_axis=0, concat_axis=0, tiled=True,...]
    all_to_all x1 -> x0, waiting for transfers between devices: 7.67 us -> none  [per_device(): lax.all_to_all(summed.reshape(experts, CAP, width), 'expert', split_axis=...]
    unnamed x20 -> x14, local copies, waits for them, and re-layouts: 7.47 us -> 1.03 us
    all_to_all x1 -> x0, starting transfers between devices: 3.51 us -> none  [per_device(): lax.all_to_all(summed.reshape(experts, CAP, width), 'expert', split_axis=...]
    pallas_call x3 -> x7, Pallas kernels: 2.39 us -> 4.55 us  [the longest x1 1.88 us: per_device(): send = serve(other, w_in[0], w_out[0])]
    ppermute x1, waiting for transfers between devices: 1.39 us -> 0.01 us  [per_device(): lax.ppermute(send, 'dp', swap)]
    reshape x4 -> x0, local copies, waits for them, and re-layouts: 0.84 us -> none  [the longest x1 0.71 us: per_device(): summed.reshape(experts, CAP, width)]
  transfers between devices with their start and end apart: 3 -> 2, of which waited for: 3 -> 1; matrix products, arithmetic and copies ran while one was open for 0% -> 0% of each run, Pallas kernels for 1% -> 7%
where the time goes in v2:
time: 33.2 us; the launch traced here: 33 us
  blocking collectives  23.8 us (72%)
  Pallas kernels  5.78 us (17%)
  waiting for transfers between devices  1.35 us (4%)
  local copies, waits for them, and re-layouts  1.03 us (3%)
  between operations  0.76 us (2%)
    all_to_all x2, blocking collectives, exchange(): lax.all_to_all(blocks, 'expert', split_axis=0, concat_axis=0, tiled=True,...  23.8 us
    pallas_call x1, Pallas kernels, per_device(): send = serve(other, w_in[0], w_out[0])  1.88 us
    pallas_call x1, Pallas kernels, per_device(): keep = serve(own, w_in[0], w_out[0])  1.88 us
    ppermute x1, waiting for transfers between devices, per_device(): other = lax.ppermute(own, 'dp', swap)  1.35 us
    pallas_call x1, Pallas kernels, per_device(): pl.pallas_call(combine_body, grid=(count // block,), in_specs=[pl.BlockSp...  1.24 us
    unnamed x14, local copies, waits for them, and re-layouts  1.03 us
  transfers between devices with their start and end apart: 2, of which 1 were waited for; matrix products, arithmetic and copies ran while one was open for 0% of the time, Pallas kernels for 7%

profile of v2, /device:TPU:0, one launch (start us, length us, event | category | flops | bytes accessed | tf_op | source)
XLA Modules:
  0.0 33.0 jit_solution(13361667420130335859)
XLA Ops:
  0.6 0.0 copy-start.2
  0.6 0.0 copy-start.5
  0.7 0.0 copy-start.4
  0.7 0.0 copy-start.6
  0.7 1.0 %copy-done.2 = bf16[256,1024]{1,0:T(8,128)(2,1)S(1)} copy-done((bf16[256,1024]{1,0:T(8,128)(2,1)S(1)}, bf16[256,1024]{1,0:T(8,128)(2,1)}, u32[]{:S(2)}) %copy-start.2) | copy-done | bytes 524312
  1.7 0.0 copy-done.5
  1.7 0.0 copy-done.4
  1.7 0.2 select.1.values_ref
  1.9 0.0 copy-done.6
  1.9 0.0 copy-start
  1.9 0.0 copy-start.1
  1.9 0.2 norm.1.normed_ref
  2.2 13.6 %all_to_all.10.rows_ref = bf16[16,4,1024]{2,1,0:T(4,128)(2,1)S(1)} all-to-all(bf16[16,4,1024]{2,1,0:T(4,128)(2,1)S(1)} %norm.1.normed_ref), channel_id=1, replica_groups={{10,11,12,13,14,15,0,1,2,3,4,5,6,7,8,9},{26,27,28,29,30,31,16,17,18,19,..., dimensions={0} | all-to-all | bytes 262144 | tf_op jit(solution)/shard_map/all_to_all | solution.py:112
  15.8 0.0 collective-permute-start
  15.8 1.3 %collective-permute-done.rows_ref = bf16[16,4,1024]{2,1,0:T(4,128)(2,1)S(1)} collective-permute-done((bf16[16,4,1024]{2,1,0:T(4,128)(2,1)S(1)}, bf16[16,4,1024]{2,1,0:T(4,128)(2,1)S(1)}, u32[]{:S(2)}, u32[]{:S(2)}) %collective-permute-start) | collective-permute-done | bytes 131104 | tf_op jit(solution)/shard_map/ppermute | solution.py:149
  17.1 0.0 copy-done
  17.1 0.0 copy-done.1
  17.1 1.9 %experts.2.after_ref = f32[64,1024]{1,0:T(8,128)S(1)} custom-call(bf16[16,4,1024]{2,1,0:T(4,128)(2,1)S(1)} %collective-permute-done.rows_ref, bf16[1024,2048]{1,0:T(8,128)(2,1)S(1)} %bitcast.6, bf16[2048,1024]{1,0:T(8,128)(2,1)S(1)} %bitcast.8), custom_call_target="tpu_custom_call" | custom-call | tf_op jit(solution)/shard_map/experts/pallas_call | solution.py:157
  19.0 0.0 copy-start.3
  19.0 0.2 collective-permute-start.1
  19.2 1.9 %experts.3.keep_ref = f32[64,1024]{1,0:T(8,128)S(1)} custom-call(bf16[16,4,1024]{2,1,0:T(4,128)(2,1)S(1)} %all_to_all.10.rows_ref, bf16[1024,2048]{1,0:T(8,128)(2,1)S(1)} %bitcast.7, bf16[2048,1024]{1,0:T(8,128)(2,1)S(1)} %bitcast.9), custom_call_target="tpu_custom_call" | custom-call | tf_op jit(solution)/shard_map/experts/pallas_call | solution.py:156
  21.1 0.0 copy-done.3
  21.1 0.3 gate.1
  21.4 0.0 collective-permute-done.1.other_ref
  21.4 0.1 join.1
  21.5 10.2 %all_to_all.11.back_ref = bf16[16,4,1024]{2,1,0:T(4,128)(2,1)S(1)} all-to-all(bf16[16,4,1024]{2,1,0:T(4,128)(2,1)S(1)} %join.1), channel_id=1, replica_groups={{10,11,12,13,14,15,0,1,2,3,4,5,6,7,8,9},{26,27,28,29,30,31,16,17,18,19,..., dimensions={0} | all-to-all | bytes 262144 | tf_op jit(solution)/shard_map/all_to_all | solution.py:112
  31.7 1.2 %combine.1 = (bf16[256,1024]{1,0:T(8,128)(2,1)}, bf16[256,1024]{1,0:T(8,128)(2,1)}) custom-call(bf16[256,1024]{1,0:T(8,128)(2,1)S(1)} %copy-done.2, bf16[256,64]{1,0:T(8,128)(2,1)S(1)} %get-tuple-element.4.pick_ref, f32[256,128]{1,0:T(8,128)S(1)} %get-tuple-element.5.after_ref.gate_ref, bf16[16,4,1024]{2,1,0:T(4,128)(2,1)S(1)} %all_to_all.11.back_ref), custom_call_target="tpu_custom_call" | custom-call | tf_op jit(solution)/shard_map/combine/pallas_call | solution.py:177
  (1 shorter events, 0.0 us)
Async XLA Ops:
  0.6 1.0 %copy-start.2 = (bf16[256,1024]{1,0:T(8,128)(2,1)S(1)}, bf16[256,1024]{1,0:T(8,128)(2,1)}, u32[]{:S(2)}) copy-start(bf16[256,1024]{1,0:T(8,128)(2,1)} %tokens_ref.3) | copy-start | bytes 1572868
  0.6 1.0 %copy-start.5 = (s32[256]{0:T(256)S(1)}, s32[256]{0:T(256)}, u32[]{:S(2)}) copy-start(s32[256]{0:T(256)} %param.11) | copy-start | bytes 3076
  0.7 1.0 %copy-start.4 = (s32[256]{0:T(256)S(1)}, s32[256]{0:T(256)}, u32[]{:S(2)}) copy-start(s32[256]{0:T(256)} %param.10) | copy-start | bytes 3076
  0.7 1.2 %copy-start.6 = (f32[1024]{0:T(1024)S(1)}, f32[1024]{0:T(1024)}, u32[]{:S(2)}) copy-start(f32[1024]{0:T(1024)} %param.8) | copy-start | bytes 12292
  1.9 15.2 %copy-start = (bf16[1,1024,2048]{2,1,0:T(8,128)(2,1)S(1)}, bf16[1,1024,2048]{2,1,0:T(8,128)(2,1)}, u32[]{:S(2)}) copy-start(bf16[1,1024,2048]{2,1,0:T(8,128)(2,1)} %param.12) | copy-start | bytes 12582916
  1.9 15.2 %copy-start.1 = (bf16[1,2048,1024]{2,1,0:T(8,128)(2,1)S(1)}, bf16[1,2048,1024]{2,1,0:T(8,128)(2,1)}, u32[]{:S(2)}) copy-start(bf16[1,2048,1024]{2,1,0:T(8,128)(2,1)} %param.13) | copy-start | bytes 12582916
  15.8 1.3 %collective-permute-start = (bf16[16,4,1024]{2,1,0:T(4,128)(2,1)S(1)}, bf16[16,4,1024]{2,1,0:T(4,128)(2,1)S(1)}, u32[]{:S(2)}, u32[]{:S(2)}) collective-permute-start(bf16[16,4,1024]{2,1,0:T(4,128)(2,1)S(1)} %all_to_all.10.rows_ref), channel_id=1, source_target_pairs={{0,16},{16,0},{1,17},{17,1},{2,18},{18,2},{3,19},{19,3},{4,20},{20... | collective-permute-start | bytes 393224 | tf_op jit(solution)/shard_map/ppermute | solution.py:149
  19.0 2.1 %copy-start.3 = (bf16[1024,16]{0,1:T(8,128)(2,1)S(1)}, bf16[1024,16]{0,1:T(8,128)(2,1)}, u32[]{:S(2)}) copy-start(bf16[1024,16]{0,1:T(8,128)(2,1)} %param.9) | copy-start | bytes 98308
  19.0 2.4 %collective-permute-start.1 = (f32[64,1024]{1,0:T(8,128)S(1)}, f32[64,1024]{1,0:T(8,128)S(1)}, u32[]{:S(2)}, u32[]{:S(2)}) collective-permute-start(f32[64,1024]{1,0:T(8,128)S(1)} %experts.2.after_ref), channel_id=1, source_target_pairs={{0,16},{16,0},{1,17},{17,1},{2,18},{18,2},{3,19},{19,3},{4,20},{20... | collective-permute-start | bytes 786440 | tf_op jit(solution)/shard_map/ppermute | solution.py:174

commit v3 on v2

--- a/solution.py
+++ b/solution.py
@@ -1,5 +1,3 @@
-import functools
-
 import jax
 import jax.numpy as jnp
 from jax import lax
@@ -10,6 +8,7 @@
 CAP = 4
 EPS = 1e-06
 MIB = 1024 * 1024
+PIECES = 4
 
 
 def rotation(count):
@@ -73,19 +72,16 @@
     return 0.5 * v * (1.0 + jnp.tanh(inner))
 
 
-def expert_body(rows_ref, w_in_ref, w_out_ref, out_ref, *, chunk):
-    rows = rows_ref[...].reshape(out_ref.shape)
-    total = None
-    for start in range(0, w_in_ref.shape[1], chunk):
-        hidden = jnp.dot(
-            rows, w_in_ref[:, start : start + chunk], preferred_element_type=jnp.float32
-        )
-        hidden = gelu(hidden).astype(jnp.bfloat16)
-        part = jnp.dot(
-            hidden, w_out_ref[start : start + chunk, :], preferred_element_type=jnp.float32
-        )
-        total = part if total is None else total + part
-    out_ref[...] = total
+def expert_body(own_ref, other_ref, w_in_ref, w_out_ref, keep_ref, send_ref):
+    own = own_ref[...].reshape(keep_ref.shape)
+    other = other_ref[...].reshape(send_ref.shape)
+    rows = jnp.concatenate([own, other], axis=0)
+    hidden = gelu(jnp.dot(rows, w_in_ref[...], preferred_element_type=jnp.float32))
+    total = jnp.dot(
+        hidden.astype(jnp.bfloat16), w_out_ref[...], preferred_element_type=jnp.float32
+    )
+    keep_ref[...] = total[: own.shape[0]]
+    send_ref[...] = total[own.shape[0] :]
 
 
 def join_body(keep_ref, other_ref, after_ref, out_ref):
@@ -94,12 +90,28 @@
     out_ref[...] = total.reshape(out_ref.shape).astype(jnp.bfloat16)
 
 
-def combine_body(tokens_ref, pick_ref, gate_ref, back_ref, mixed_ref, update_ref):
+def combine_body(
+    tokens_ref, pick_ref, gate_ref, back_ref, mixed_hbm, update_hbm, mixed, update, sems
+):
     back = back_ref[...].reshape(pick_ref.shape[1], back_ref.shape[2])
-    update = jnp.dot(pick_ref[...], back, preferred_element_type=jnp.float32)
-    update_ref[...] = update.astype(jnp.bfloat16)
-    mixed = tokens_ref[...].astype(jnp.float32) + gate_ref[:, :1] * update
-    mixed_ref[...] = mixed.astype(jnp.bfloat16)
+    block = tokens_ref.shape[0] // PIECES
+    copies = []
+    for piece in range(PIECES):
+        rows = pl.ds(piece * block, block)
+        value = jnp.dot(pick_ref[rows, :], back, preferred_element_type=jnp.float32)
+        update[rows, :] = value.astype(jnp.bfloat16)
+        copies.append(
+            pltpu.make_async_copy(update.at[rows], update_hbm.at[rows], sems.at[0, piece])
+        )
+        copies[-1].start()
+        value = tokens_ref[rows, :].astype(jnp.float32) + gate_ref[rows, :1] * value
+        mixed[rows, :] = value.astype(jnp.bfloat16)
+        copies.append(
+            pltpu.make_async_copy(mixed.at[rows], mixed_hbm.at[rows], sems.at[1, piece])
+        )
+        copies[-1].start()
+    for copy in copies:
+        copy.wait()
 
 
 def params(limit):
@@ -147,14 +159,15 @@
     )(values, ln_gain.reshape(1, width))
     own = exchange(outgoing)
     other = lax.ppermute(own, "dp", swap)
-    serve = pl.pallas_call(
-        functools.partial(expert_body, chunk=512),
-        out_shape=jax.ShapeDtypeStruct((slots, width), jnp.float32),
+    keep, send = pl.pallas_call(
+        expert_body,
+        out_shape=(
+            jax.ShapeDtypeStruct((slots, width), jnp.float32),
+            jax.ShapeDtypeStruct((slots, width), jnp.float32),
+        ),
         compiler_params=params(24),
         name="experts",
-    )
-    keep = serve(own, w_in[0], w_out[0])
-    send = serve(other, w_in[0], w_out[0])
+    )(own, other, w_in[0], w_out[0])
     pick, gate = pl.pallas_call(
         gate_body,
         in_specs=[whole] * 4 + [anywhere],
@@ -173,19 +186,14 @@
         name="join",
     )(keep, lax.ppermute(send, "dp", swap), gate)
     back = exchange(summed)
-    block = count // 2
     mixed, update = pl.pallas_call(
         combine_body,
-        grid=(count // block,),
-        in_specs=[
-            pl.BlockSpec((block, width), lambda i: (i, 0)),
-            pl.BlockSpec((block, slots), lambda i: (i, 0)),
-            pl.BlockSpec((block, 128), lambda i: (i, 0)),
-            pl.BlockSpec((experts, CAP, width), lambda i: (0, 0, 0)),
-        ],
-        out_specs=[
-            pl.BlockSpec((block, width), lambda i: (i, 0)),
-            pl.BlockSpec((block, width), lambda i: (i, 0)),
+        in_specs=[whole] * 4,
+        out_specs=[anywhere] * 2,
+        scratch_shapes=[
+            pltpu.VMEM((count, width), jnp.bfloat16),
+            pltpu.VMEM((count, width), jnp.bfloat16),
+            pltpu.SemaphoreType.DMA((2, PIECES)),
         ],
         out_shape=(
             jax.ShapeDtypeStruct((count, width), jnp.bfloat16),

time: 33.2 us -> 31.7 us (0.955)
  Pallas kernels: 5.78 us -> 3.43 us
  waiting for transfers between devices: 1.35 us -> 2.43 us
    pallas_call x3 -> x2, Pallas kernels: 5 us -> 2.65 us  [the longest x1 1.44 us: per_device(): pl.pallas_call(expert_body, out_shape=(jax.ShapeDtypeStruct((slots, width...]
    ppermute x1, waiting for transfers between devices: 0.01 us -> 1.09 us  [per_device(): lax.ppermute(send, 'dp', swap)]
  transfers between devices with their start and end apart: 2 -> 2, of which waited for: 1 -> 2; matrix products, arithmetic and copies ran while one was open for 0% -> 0% of each run, Pallas kernels for 7% -> 1%
where the time goes in v3:
time: 31.7 us; the launch traced here: 31.5 us
  blocking collectives  23.7 us (75%)
  Pallas kernels  3.43 us (11%)
  waiting for transfers between devices  2.43 us (8%)
  local copies, waits for them, and re-layouts  1.02 us (3%)
  between operations  0.73 us (2%)
    all_to_all x2, blocking collectives, exchange(): lax.all_to_all(blocks, 'expert', split_axis=0, concat_axis=0, tiled=True,...  23.7 us
    pallas_call x1, Pallas kernels, per_device(): pl.pallas_call(expert_body, out_shape=(jax.ShapeDtypeStruct((slots, width...  1.44 us
    ppermute x1, waiting for transfers between devices, per_device(): other = lax.ppermute(own, 'dp', swap)  1.35 us
    pallas_call x1, Pallas kernels, per_device(): pl.pallas_call(combine_body, in_specs=[whole] * 4, out_specs=[anywhere] *...  1.2 us
    ppermute x1, waiting for transfers between devices, per_device(): lax.ppermute(send, 'dp', swap)  1.09 us
    unnamed x14, local copies, waits for them, and re-layouts  1.02 us
  transfers between devices with their start and end apart: 2, of which 2 were waited for; matrix products, arithmetic and copies ran while one was open for 0% of the time, Pallas kernels for 1%

profile of v3, /device:TPU:0, one launch (start us, length us, event | category | flops | bytes accessed | tf_op | source)
XLA Modules:
  0.0 31.5 jit_solution(12895534370457602163)
XLA Ops:
  0.6 0.0 copy-start.2
  0.6 0.0 copy-start.5
  0.7 0.0 copy-start.4
  0.7 0.0 copy-start.6
  0.7 1.0 %copy-done.2 = bf16[256,1024]{1,0:T(8,128)(2,1)S(1)} copy-done((bf16[256,1024]{1,0:T(8,128)(2,1)S(1)}, bf16[256,1024]{1,0:T(8,128)(2,1)}, u32[]{:S(2)}) %copy-start.2) | copy-done | bytes 524312
  1.7 0.0 copy-done.5
  1.7 0.0 copy-done.4
  1.7 0.2 select.1.values_ref
  1.9 0.0 copy-done.6
  1.9 0.0 copy-start
  1.9 0.0 copy-start.1
  1.9 0.2 norm.1.normed_ref
  2.2 13.6 %all_to_all.10.own_ref = bf16[16,4,1024]{2,1,0:T(4,128)(2,1)S(1)} all-to-all(bf16[16,4,1024]{2,1,0:T(4,128)(2,1)S(1)} %norm.1.normed_ref), channel_id=1, replica_groups={{10,11,12,13,14,15,0,1,2,3,4,5,6,7,8,9},{26,27,28,29,30,31,16,17,18,19,..., dimensions={0} | all-to-all | bytes 262144 | tf_op jit(solution)/shard_map/all_to_all | solution.py:124
  15.8 0.0 collective-permute-start
  15.8 1.3 %collective-permute-done.other_ref = bf16[16,4,1024]{2,1,0:T(4,128)(2,1)S(1)} collective-permute-done((bf16[16,4,1024]{2,1,0:T(4,128)(2,1)S(1)}, bf16[16,4,1024]{2,1,0:T(4,128)(2,1)S(1)}, u32[]{:S(2)}, u32[]{:S(2)}) %collective-permute-start) | collective-permute-done | bytes 131104 | tf_op jit(solution)/shard_map/ppermute | solution.py:161
  17.1 0.0 copy-done
  17.1 0.0 copy-done.1
  17.1 0.0 copy-start.3
  17.1 1.4 %experts.1 = (f32[64,1024]{1,0:T(8,128)S(1)}, f32[64,1024]{1,0:T(8,128)S(1)}) custom-call(bf16[16,4,1024]{2,1,0:T(4,128)(2,1)S(1)} %all_to_all.10.own_ref, bf16[16,4,1024]{2,1,0:T(4,128)(2,1)S(1)} %collective-permute-done.other_ref, bf16[1024,2048]{1,0:T(8,128)(2,1)S(1)} %bitcast.6, bf16[2048,1024]{1,0:T(8,128)(2,1)S(1)} %bitcast.7), custom_call_target="tpu_custom_call" | custom-call | tf_op jit(solution)/shard_map/experts/pallas_call | solution.py:162
  18.6 0.2 collective-permute-start.1
  18.8 0.0 copy-done.3
  18.8 0.3 gate.1
  19.1 1.1 %collective-permute-done.1.other_ref = f32[64,1024]{1,0:T(8,128)S(1)} collective-permute-done((f32[64,1024]{1,0:T(8,128)S(1)}, f32[64,1024]{1,0:T(8,128)S(1)}, u32[]{:S(2)}, u32[]{:S(2)}) %collective-permute-start.1) | collective-permute-done | bytes 262176 | tf_op jit(solution)/shard_map/ppermute | solution.py:187
  20.2 0.1 join.1
  20.2 10.1 %all_to_all.11.back_ref = bf16[16,4,1024]{2,1,0:T(4,128)(2,1)S(1)} all-to-all(bf16[16,4,1024]{2,1,0:T(4,128)(2,1)S(1)} %join.1), channel_id=1, replica_groups={{10,11,12,13,14,15,0,1,2,3,4,5,6,7,8,9},{26,27,28,29,30,31,16,17,18,19,..., dimensions={0} | all-to-all | bytes 262144 | tf_op jit(solution)/shard_map/all_to_all | solution.py:124
  30.3 1.2 %combine.1 = (bf16[256,1024]{1,0:T(8,128)(2,1)}, bf16[256,1024]{1,0:T(8,128)(2,1)}) custom-call(bf16[256,1024]{1,0:T(8,128)(2,1)S(1)} %copy-done.2, bf16[256,64]{1,0:T(8,128)(2,1)S(1)} %get-tuple-element.7.pick_ref, f32[256,128]{1,0:T(8,128)S(1)} %get-tuple-element.8.after_ref.gate_ref, bf16[16,4,1024]{2,1,0:T(4,128)(2,1)S(1)} %all_to_all.11.back_ref), custom_call_target="tpu_custom_call" | custom-call | tf_op jit(solution)/shard_map/combine/pallas_call | solution.py:189
  (1 shorter events, 0.0 us)
Async XLA Ops:
  0.6 1.0 %copy-start.2 = (bf16[256,1024]{1,0:T(8,128)(2,1)S(1)}, bf16[256,1024]{1,0:T(8,128)(2,1)}, u32[]{:S(2)}) copy-start(bf16[256,1024]{1,0:T(8,128)(2,1)} %tokens_ref.3) | copy-start | bytes 1572868
  0.6 1.0 %copy-start.5 = (s32[256]{0:T(256)S(1)}, s32[256]{0:T(256)}, u32[]{:S(2)}) copy-start(s32[256]{0:T(256)} %param.11) | copy-start | bytes 3076
  0.7 1.0 %copy-start.4 = (s32[256]{0:T(256)S(1)}, s32[256]{0:T(256)}, u32[]{:S(2)}) copy-start(s32[256]{0:T(256)} %param.10) | copy-start | bytes 3076
  0.7 1.2 %copy-start.6 = (f32[1024]{0:T(1024)S(1)}, f32[1024]{0:T(1024)}, u32[]{:S(2)}) copy-start(f32[1024]{0:T(1024)} %param.8) | copy-start | bytes 12292
  1.9 15.2 %copy-start = (bf16[1,1024,2048]{2,1,0:T(8,128)(2,1)S(1)}, bf16[1,1024,2048]{2,1,0:T(8,128)(2,1)}, u32[]{:S(2)}) copy-start(bf16[1,1024,2048]{2,1,0:T(8,128)(2,1)} %param.12) | copy-start | bytes 12582916
  1.9 15.2 %copy-start.1 = (bf16[1,2048,1024]{2,1,0:T(8,128)(2,1)S(1)}, bf16[1,2048,1024]{2,1,0:T(8,128)(2,1)}, u32[]{:S(2)}) copy-start(bf16[1,2048,1024]{2,1,0:T(8,128)(2,1)} %param.13) | copy-start | bytes 12582916
  15.8 1.3 %collective-permute-start = (bf16[16,4,1024]{2,1,0:T(4,128)(2,1)S(1)}, bf16[16,4,1024]{2,1,0:T(4,128)(2,1)S(1)}, u32[]{:S(2)}, u32[]{:S(2)}) collective-permute-start(bf16[16,4,1024]{2,1,0:T(4,128)(2,1)S(1)} %all_to_all.10.own_ref), channel_id=1, source_target_pairs={{0,16},{16,0},{1,17},{17,1},{2,18},{18,2},{3,19},{19,3},{4,20},{20... | collective-permute-start | bytes 393224 | tf_op jit(solution)/shard_map/ppermute | solution.py:161
  17.1 1.7 %copy-start.3 = (bf16[1024,16]{0,1:T(8,128)(2,1)S(1)}, bf16[1024,16]{0,1:T(8,128)(2,1)}, u32[]{:S(2)}) copy-start(bf16[1024,16]{0,1:T(8,128)(2,1)} %param.9) | copy-start | bytes 98308
  18.6 1.6 %collective-permute-start.1 = (f32[64,1024]{1,0:T(8,128)S(1)}, f32[64,1024]{1,0:T(8,128)S(1)}, u32[]{:S(2)}, u32[]{:S(2)}) collective-permute-start(f32[64,1024]{1,0:T(8,128)S(1)} %get-tuple-element.6.after_ref), channel_id=1, source_target_pairs={{0,16},{16,0},{1,17},{17,1},{2,18},{18,2},{3,19},{19,3},{4,20},{20... | collective-permute-start | bytes 786440 | tf_op jit(solution)/shard_map/ppermute | solution.py:187

commit v4 on v3

--- a/solution.py
+++ b/solution.py
@@ -120,9 +120,16 @@
 
 def exchange(blocks):
     count = blocks.shape[0]
-    group = [(i + rotation(count)) % count for i in range(count)]
+    order = [(i + rotation(count)) % count for i in range(count)]
+    near = [i + count * (i >= count // 2) for i in order]
+    far = [i + count * (i < count // 2) for i in order]
     return lax.all_to_all(
-        blocks, "expert", split_axis=0, concat_axis=0, tiled=True, axis_index_groups=[group]
+        blocks,
+        ("dp", "expert"),
+        split_axis=0,
+        concat_axis=0,
+        tiled=True,
+        axis_index_groups=[near, far],
     )
 
 

time: 31.7 us -> 31.2 us (0.984)
  blocking collectives: 23.7 us -> 22.1 us
  starting transfers between devices: 0.22 us -> 1.57 us
  waiting for transfers between devices: 2.43 us -> 1.85 us
    all_to_all x2, blocking collectives: 23.7 us -> 22.1 us  [exchange(): lax.all_to_all(blocks, ('dp', 'expert'), split_axis=0, concat_axis=0, til...]
    ppermute x1, starting transfers between devices: 0.01 us -> 1.13 us  [per_device(): other = lax.ppermute(own, 'dp', swap)]
    ppermute x1, waiting for transfers between devices: 1.35 us -> 0.99 us  [per_device(): other = lax.ppermute(own, 'dp', swap)]
where the time goes in v4:
time: 31.2 us; the launch traced here: 30.7 us
  blocking collectives  22.1 us (71%)
  Pallas kernels  3.43 us (11%)
  waiting for transfers between devices  1.85 us (6%)
  starting transfers between devices  1.57 us (5%)
  local copies, waits for them, and re-layouts  1.02 us (3%)
  between operations  0.73 us (2%)
    all_to_all x2, blocking collectives, exchange(): lax.all_to_all(blocks, ('dp', 'expert'), split_axis=0, concat_axis=0, til...  22.1 us
    pallas_call x1, Pallas kernels, per_device(): pl.pallas_call(expert_body, out_shape=(jax.ShapeDtypeStruct((slots, width...  1.44 us
    pallas_call x1, Pallas kernels, per_device(): pl.pallas_call(combine_body, in_specs=[whole] * 4, out_specs=[anywhere] *...  1.2 us
    ppermute x1, starting transfers between devices, per_device(): other = lax.ppermute(own, 'dp', swap)  1.13 us
    unnamed x14, local copies, waits for them, and re-layouts  1.02 us
    ppermute x1, waiting for transfers between devices, per_device(): other = lax.ppermute(own, 'dp', swap)  0.99 us
    ppermute x1, waiting for transfers between devices, per_device(): lax.ppermute(send, 'dp', swap)  0.86 us
  transfers between devices with their start and end apart: 2, of which 2 were waited for; matrix products, arithmetic and copies ran while one was open for 0% of the time, Pallas kernels for 1%

profile of v4, /device:TPU:0, one launch (start us, length us, event | category | flops | bytes accessed | tf_op | source)
XLA Modules:
  0.0 30.7 jit_solution(8031077169988039104)
XLA Ops:
  0.6 0.0 copy-start.2
  0.6 0.0 copy-start.5
  0.7 0.0 copy-start.4
  0.7 0.0 copy-start.6
  0.7 1.0 %copy-done.2 = bf16[256,1024]{1,0:T(8,128)(2,1)S(1)} copy-done((bf16[256,1024]{1,0:T(8,128)(2,1)S(1)}, bf16[256,1024]{1,0:T(8,128)(2,1)}, u32[]{:S(2)}) %copy-start.2) | copy-done | bytes 524312
  1.7 0.0 copy-done.5
  1.7 0.0 copy-done.4
  1.7 0.2 select.1.values_ref
  1.9 0.0 copy-done.6
  1.9 0.0 copy-start
  1.9 0.0 copy-start.1
  1.9 0.2 norm.1.normed_ref
  2.2 12.3 %all_to_all.10.own_ref = bf16[16,4,1024]{2,1,0:T(4,128)(2,1)S(1)} all-to-all(bf16[16,4,1024]{2,1,0:T(4,128)(2,1)S(1)} %norm.1.normed_ref), channel_id=1, replica_groups={{26,27,28,29,30,31,0,1,2,3,4,5,6,7,24,25},{10,11,12,13,14,15,16,17,18,1..., dimensions={0} | all-to-all | bytes 262144 | tf_op jit(solution)/shard_map/all_to_all | solution.py:126
  14.4 1.1 %collective-permute-start = (bf16[16,4,1024]{2,1,0:T(4,128)(2,1)S(1)}, bf16[16,4,1024]{2,1,0:T(4,128)(2,1)S(1)}, u32[]{:S(2)}, u32[]{:S(2)}) collective-permute-start(bf16[16,4,1024]{2,1,0:T(4,128)(2,1)S(1)} %all_to_all.10.own_ref), channel_id=1, source_target_pairs={{0,16},{16,0},{1,17},{17,1},{2,18},{18,2},{3,19},{19,3},{4,20},{20... | collective-permute-start | bytes 393224 | tf_op jit(solution)/shard_map/ppermute | solution.py:168
  15.6 1.0 %collective-permute-done.other_ref = bf16[16,4,1024]{2,1,0:T(4,128)(2,1)S(1)} collective-permute-done((bf16[16,4,1024]{2,1,0:T(4,128)(2,1)S(1)}, bf16[16,4,1024]{2,1,0:T(4,128)(2,1)S(1)}, u32[]{:S(2)}, u32[]{:S(2)}) %collective-permute-start) | collective-permute-done | bytes 131104 | tf_op jit(solution)/shard_map/ppermute | solution.py:168
  16.6 0.0 copy-done
  16.6 0.0 copy-done.1
  16.6 0.0 copy-start.3
  16.6 1.4 %experts.1 = (f32[64,1024]{1,0:T(8,128)S(1)}, f32[64,1024]{1,0:T(8,128)S(1)}) custom-call(bf16[16,4,1024]{2,1,0:T(4,128)(2,1)S(1)} %all_to_all.10.own_ref, bf16[16,4,1024]{2,1,0:T(4,128)(2,1)S(1)} %collective-permute-done.other_ref, bf16[1024,2048]{1,0:T(8,128)(2,1)S(1)} %bitcast.6, bf16[2048,1024]{1,0:T(8,128)(2,1)S(1)} %bitcast.7), custom_call_target="tpu_custom_call" | custom-call | tf_op jit(solution)/shard_map/experts/pallas_call | solution.py:169
  18.0 0.4 %collective-permute-start.1 = (f32[64,1024]{1,0:T(8,128)S(1)}, f32[64,1024]{1,0:T(8,128)S(1)}, u32[]{:S(2)}, u32[]{:S(2)}) collective-permute-start(f32[64,1024]{1,0:T(8,128)S(1)} %get-tuple-element.6.after_ref), channel_id=1, source_target_pairs={{0,16},{16,0},{1,17},{17,1},{2,18},{18,2},{3,19},{19,3},{4,20},{20... | collective-permute-start | bytes 786440 | tf_op jit(solution)/shard_map/ppermute | solution.py:194
  18.5 0.0 copy-done.3
  18.5 0.3 gate.1
  18.8 0.9 %collective-permute-done.1.other_ref = f32[64,1024]{1,0:T(8,128)S(1)} collective-permute-done((f32[64,1024]{1,0:T(8,128)S(1)}, f32[64,1024]{1,0:T(8,128)S(1)}, u32[]{:S(2)}, u32[]{:S(2)}) %collective-permute-start.1) | collective-permute-done | bytes 262176 | tf_op jit(solution)/shard_map/ppermute | solution.py:194
  19.6 0.1 join.1
  19.7 9.9 %all_to_all.11.back_ref = bf16[16,4,1024]{2,1,0:T(4,128)(2,1)S(1)} all-to-all(bf16[16,4,1024]{2,1,0:T(4,128)(2,1)S(1)} %join.1), channel_id=1, replica_groups={{26,27,28,29,30,31,0,1,2,3,4,5,6,7,24,25},{10,11,12,13,14,15,16,17,18,1..., dimensions={0} | all-to-all | bytes 262144 | tf_op jit(solution)/shard_map/all_to_all | solution.py:126
  29.5 1.2 %combine.1 = (bf16[256,1024]{1,0:T(8,128)(2,1)}, bf16[256,1024]{1,0:T(8,128)(2,1)}) custom-call(bf16[256,1024]{1,0:T(8,128)(2,1)S(1)} %copy-done.2, bf16[256,64]{1,0:T(8,128)(2,1)S(1)} %get-tuple-element.7.pick_ref, f32[256,128]{1,0:T(8,128)S(1)} %get-tuple-element.8.after_ref.gate_ref, bf16[16,4,1024]{2,1,0:T(4,128)(2,1)S(1)} %all_to_all.11.back_ref), custom_call_target="tpu_custom_call" | custom-call | tf_op jit(solution)/shard_map/combine/pallas_call | solution.py:196
  (1 shorter events, 0.0 us)
Async XLA Ops:
  0.6 1.0 %copy-start.2 = (bf16[256,1024]{1,0:T(8,128)(2,1)S(1)}, bf16[256,1024]{1,0:T(8,128)(2,1)}, u32[]{:S(2)}) copy-start(bf16[256,1024]{1,0:T(8,128)(2,1)} %tokens_ref.3) | copy-start | bytes 1572868
  0.6 1.0 %copy-start.5 = (s32[256]{0:T(256)S(1)}, s32[256]{0:T(256)}, u32[]{:S(2)}) copy-start(s32[256]{0:T(256)} %param.11) | copy-start | bytes 3076
  0.7 1.0 %copy-start.4 = (s32[256]{0:T(256)S(1)}, s32[256]{0:T(256)}, u32[]{:S(2)}) copy-start(s32[256]{0:T(256)} %param.10) | copy-start | bytes 3076
  0.7 1.2 %copy-start.6 = (f32[1024]{0:T(1024)S(1)}, f32[1024]{0:T(1024)}, u32[]{:S(2)}) copy-start(f32[1024]{0:T(1024)} %param.8) | copy-start | bytes 12292
  1.9 14.7 %copy-start = (bf16[1,1024,2048]{2,1,0:T(8,128)(2,1)S(1)}, bf16[1,1024,2048]{2,1,0:T(8,128)(2,1)}, u32[]{:S(2)}) copy-start(bf16[1,1024,2048]{2,1,0:T(8,128)(2,1)} %param.12) | copy-start | bytes 12582916
  1.9 14.7 %copy-start.1 = (bf16[1,2048,1024]{2,1,0:T(8,128)(2,1)S(1)}, bf16[1,2048,1024]{2,1,0:T(8,128)(2,1)}, u32[]{:S(2)}) copy-start(bf16[1,2048,1024]{2,1,0:T(8,128)(2,1)} %param.13) | copy-start | bytes 12582916
  14.4 2.1 %collective-permute-start = (bf16[16,4,1024]{2,1,0:T(4,128)(2,1)S(1)}, bf16[16,4,1024]{2,1,0:T(4,128)(2,1)S(1)}, u32[]{:S(2)}, u32[]{:S(2)}) collective-permute-start(bf16[16,4,1024]{2,1,0:T(4,128)(2,1)S(1)} %all_to_all.10.own_ref), channel_id=1, source_target_pairs={{0,16},{16,0},{1,17},{17,1},{2,18},{18,2},{3,19},{19,3},{4,20},{20... | collective-permute-start | bytes 393224 | tf_op jit(solution)/shard_map/ppermute | solution.py:168
  16.6 1.9 %copy-start.3 = (bf16[1024,16]{0,1:T(8,128)(2,1)S(1)}, bf16[1024,16]{0,1:T(8,128)(2,1)}, u32[]{:S(2)}) copy-start(bf16[1024,16]{0,1:T(8,128)(2,1)} %param.9) | copy-start | bytes 98308
  18.0 1.6 %collective-permute-start.1 = (f32[64,1024]{1,0:T(8,128)S(1)}, f32[64,1024]{1,0:T(8,128)S(1)}, u32[]{:S(2)}, u32[]{:S(2)}) collective-permute-start(f32[64,1024]{1,0:T(8,128)S(1)} %get-tuple-element.6.after_ref), channel_id=1, source_target_pairs={{0,16},{16,0},{1,17},{17,1},{2,18},{18,2},{3,19},{19,3},{4,20},{20... | collective-permute-start | bytes 786440 | tf_op jit(solution)/shard_map/ppermute | solution.py:194

commit v5 on v4

--- a/solution.py
+++ b/solution.py
@@ -81,12 +81,12 @@
         hidden.astype(jnp.bfloat16), w_out_ref[...], preferred_element_type=jnp.float32
     )
     keep_ref[...] = total[: own.shape[0]]
-    send_ref[...] = total[own.shape[0] :]
+    send_ref[...] = total[own.shape[0] :].astype(send_ref.dtype)
 
 
 def join_body(keep_ref, other_ref, after_ref, out_ref):
     del after_ref
-    total = keep_ref[...] + other_ref[...]
+    total = keep_ref[...] + other_ref[...].astype(jnp.float32)
     out_ref[...] = total.reshape(out_ref.shape).astype(jnp.bfloat16)
 
 
@@ -170,7 +170,7 @@
         expert_body,
         out_shape=(
             jax.ShapeDtypeStruct((slots, width), jnp.float32),
-            jax.ShapeDtypeStruct((slots, width), jnp.float32),
+            jax.ShapeDtypeStruct((slots, width), jnp.bfloat16),
         ),
         compiler_params=params(24),
         name="experts",

time: 31.2 us -> 31.1 us (level)
  no operation moved by 1% of the time
where the time goes in v5:
time: 31.1 us; the launch traced here: 30.6 us
  blocking collectives  22.1 us (71%)
  Pallas kernels  3.44 us (11%)
  waiting for transfers between devices  1.67 us (5%)
  starting transfers between devices  1.57 us (5%)
  local copies, waits for them, and re-layouts  1.02 us (3%)
  between operations  0.73 us (2%)
    all_to_all x2, blocking collectives, exchange(): lax.all_to_all(blocks, ('dp', 'expert'), split_axis=0, concat_axis=0, til...  22.1 us
    pallas_call x1, Pallas kernels, per_device(): pl.pallas_call(expert_body, out_shape=(jax.ShapeDtypeStruct((slots, width...  1.44 us
    pallas_call x1, Pallas kernels, per_device(): pl.pallas_call(combine_body, in_specs=[whole] * 4, out_specs=[anywhere] *...  1.21 us
    ppermute x1, starting transfers between devices, per_device(): other = lax.ppermute(own, 'dp', swap)  1.13 us
    unnamed x14, local copies, waits for them, and re-layouts  1.02 us
    ppermute x1, waiting for transfers between devices, per_device(): other = lax.ppermute(own, 'dp', swap)  0.99 us
    ppermute x1, waiting for transfers between devices, per_device(): lax.ppermute(send, 'dp', swap)  0.69 us
  transfers between devices with their start and end apart: 2, of which 2 were waited for; matrix products, arithmetic and copies ran while one was open for 0% of the time, Pallas kernels for 1%

profile of v5, /device:TPU:0, one launch (start us, length us, event | category | flops | bytes accessed | tf_op | source)
XLA Modules:
  0.0 30.6 jit_solution(13830751275349771171)
XLA Ops:
  0.6 0.0 copy-start.2
  0.6 0.0 copy-start.5
  0.7 0.0 copy-start.4
  0.7 0.0 copy-start.6
  0.7 1.0 %copy-done.2 = bf16[256,1024]{1,0:T(8,128)(2,1)S(1)} copy-done((bf16[256,1024]{1,0:T(8,128)(2,1)S(1)}, bf16[256,1024]{1,0:T(8,128)(2,1)}, u32[]{:S(2)}) %copy-start.2) | copy-done | bytes 524312
  1.7 0.0 copy-done.5
  1.7 0.0 copy-done.4
  1.7 0.2 select.1.values_ref
  1.9 0.0 copy-done.6
  1.9 0.0 copy-start
  1.9 0.0 copy-start.1
  1.9 0.2 norm.1.normed_ref
  2.2 12.3 %all_to_all.10.own_ref = bf16[16,4,1024]{2,1,0:T(4,128)(2,1)S(1)} all-to-all(bf16[16,4,1024]{2,1,0:T(4,128)(2,1)S(1)} %norm.1.normed_ref), channel_id=1, replica_groups={{26,27,28,29,30,31,0,1,2,3,4,5,6,7,24,25},{10,11,12,13,14,15,16,17,18,1..., dimensions={0} | all-to-all | bytes 262144 | tf_op jit(solution)/shard_map/all_to_all | solution.py:126
  14.4 1.1 %collective-permute-start = (bf16[16,4,1024]{2,1,0:T(4,128)(2,1)S(1)}, bf16[16,4,1024]{2,1,0:T(4,128)(2,1)S(1)}, u32[]{:S(2)}, u32[]{:S(2)}) collective-permute-start(bf16[16,4,1024]{2,1,0:T(4,128)(2,1)S(1)} %all_to_all.10.own_ref), channel_id=1, source_target_pairs={{0,16},{16,0},{1,17},{17,1},{2,18},{18,2},{3,19},{19,3},{4,20},{20... | collective-permute-start | bytes 393224 | tf_op jit(solution)/shard_map/ppermute | solution.py:168
  15.6 1.0 %collective-permute-done.other_ref = bf16[16,4,1024]{2,1,0:T(4,128)(2,1)S(1)} collective-permute-done((bf16[16,4,1024]{2,1,0:T(4,128)(2,1)S(1)}, bf16[16,4,1024]{2,1,0:T(4,128)(2,1)S(1)}, u32[]{:S(2)}, u32[]{:S(2)}) %collective-permute-start) | collective-permute-done | bytes 131104 | tf_op jit(solution)/shard_map/ppermute | solution.py:168
  16.6 0.0 copy-done
  16.6 0.0 copy-done.1
  16.6 0.0 copy-start.3
  16.6 1.4 %experts.1 = (f32[64,1024]{1,0:T(8,128)S(1)}, bf16[64,1024]{1,0:T(8,128)(2,1)S(1)}) custom-call(bf16[16,4,1024]{2,1,0:T(4,128)(2,1)S(1)} %all_to_all.10.own_ref, bf16[16,4,1024]{2,1,0:T(4,128)(2,1)S(1)} %collective-permute-done.other_ref, bf16[1024,2048]{1,0:T(8,128)(2,1)S(1)} %bitcast.6, bf16[2048,1024]{1,0:T(8,128)(2,1)S(1)} %bitcast.7), custom_call_target="tpu_custom_call" | custom-call | tf_op jit(solution)/shard_map/experts/pallas_call | solution.py:169
  18.0 0.4 %collective-permute-start.1 = (bf16[64,1024]{1,0:T(8,128)(2,1)S(1)}, bf16[64,1024]{1,0:T(8,128)(2,1)S(1)}, u32[]{:S(2)}, u32[]{:S(2)}) collective-permute-start(bf16[64,1024]{1,0:T(8,128)(2,1)S(1)} %get-tuple-element.6.after_ref), channel_id=1, source_target_pairs={{0,16},{16,0},{1,17},{17,1},{2,18},{18,2},{3,19},{19,3},{4,20},{20... | collective-permute-start | bytes 393224 | tf_op jit(solution)/shard_map/ppermute | solution.py:194
  18.5 0.0 copy-done.3
  18.5 0.3 gate.1
  18.8 0.7 %collective-permute-done.1.other_ref = bf16[64,1024]{1,0:T(8,128)(2,1)S(1)} collective-permute-done((bf16[64,1024]{1,0:T(8,128)(2,1)S(1)}, bf16[64,1024]{1,0:T(8,128)(2,1)S(1)}, u32[]{:S(2)}, u32[]{:S(2)}) %collective-permute-start.1) | collective-permute-done | bytes 131104 | tf_op jit(solution)/shard_map/ppermute | solution.py:194
  19.4 0.1 join.1
  19.5 9.9 %all_to_all.11.back_ref = bf16[16,4,1024]{2,1,0:T(4,128)(2,1)S(1)} all-to-all(bf16[16,4,1024]{2,1,0:T(4,128)(2,1)S(1)} %join.1), channel_id=1, replica_groups={{26,27,28,29,30,31,0,1,2,3,4,5,6,7,24,25},{10,11,12,13,14,15,16,17,18,1..., dimensions={0} | all-to-all | bytes 262144 | tf_op jit(solution)/shard_map/all_to_all | solution.py:126
  29.4 1.2 %combine.1 = (bf16[256,1024]{1,0:T(8,128)(2,1)}, bf16[256,1024]{1,0:T(8,128)(2,1)}) custom-call(bf16[256,1024]{1,0:T(8,128)(2,1)S(1)} %copy-done.2, bf16[256,64]{1,0:T(8,128)(2,1)S(1)} %get-tuple-element.7.pick_ref, f32[256,128]{1,0:T(8,128)S(1)} %get-tuple-element.8.after_ref.gate_ref, bf16[16,4,1024]{2,1,0:T(4,128)(2,1)S(1)} %all_to_all.11.back_ref), custom_call_target="tpu_custom_call" | custom-call | tf_op jit(solution)/shard_map/combine/pallas_call | solution.py:196
  (1 shorter events, 0.0 us)
Async XLA Ops:
  0.6 1.0 %copy-start.2 = (bf16[256,1024]{1,0:T(8,128)(2,1)S(1)}, bf16[256,1024]{1,0:T(8,128)(2,1)}, u32[]{:S(2)}) copy-start(bf16[256,1024]{1,0:T(8,128)(2,1)} %tokens_ref.3) | copy-start | bytes 1572868
  0.6 1.0 %copy-start.5 = (s32[256]{0:T(256)S(1)}, s32[256]{0:T(256)}, u32[]{:S(2)}) copy-start(s32[256]{0:T(256)} %param.11) | copy-start | bytes 3076
  0.7 1.0 %copy-start.4 = (s32[256]{0:T(256)S(1)}, s32[256]{0:T(256)}, u32[]{:S(2)}) copy-start(s32[256]{0:T(256)} %param.10) | copy-start | bytes 3076
  0.7 1.2 %copy-start.6 = (f32[1024]{0:T(1024)S(1)}, f32[1024]{0:T(1024)}, u32[]{:S(2)}) copy-start(f32[1024]{0:T(1024)} %param.8) | copy-start | bytes 12292
  1.9 14.7 %copy-start = (bf16[1,1024,2048]{2,1,0:T(8,128)(2,1)S(1)}, bf16[1,1024,2048]{2,1,0:T(8,128)(2,1)}, u32[]{:S(2)}) copy-start(bf16[1,1024,2048]{2,1,0:T(8,128)(2,1)} %param.12) | copy-start | bytes 12582916
  1.9 14.7 %copy-start.1 = (bf16[1,2048,1024]{2,1,0:T(8,128)(2,1)S(1)}, bf16[1,2048,1024]{2,1,0:T(8,128)(2,1)}, u32[]{:S(2)}) copy-start(bf16[1,2048,1024]{2,1,0:T(8,128)(2,1)} %param.13) | copy-start | bytes 12582916
  14.4 2.1 %collective-permute-start = (bf16[16,4,1024]{2,1,0:T(4,128)(2,1)S(1)}, bf16[16,4,1024]{2,1,0:T(4,128)(2,1)S(1)}, u32[]{:S(2)}, u32[]{:S(2)}) collective-permute-start(bf16[16,4,1024]{2,1,0:T(4,128)(2,1)S(1)} %all_to_all.10.own_ref), channel_id=1, source_target_pairs={{0,16},{16,0},{1,17},{17,1},{2,18},{18,2},{3,19},{19,3},{4,20},{20... | collective-permute-start | bytes 393224 | tf_op jit(solution)/shard_map/ppermute | solution.py:168
  16.6 1.9 %copy-start.3 = (bf16[1024,16]{0,1:T(8,128)(2,1)S(1)}, bf16[1024,16]{0,1:T(8,128)(2,1)}, u32[]{:S(2)}) copy-start(bf16[1024,16]{0,1:T(8,128)(2,1)} %param.9) | copy-start | bytes 98308
  18.0 1.4 %collective-permute-start.1 = (bf16[64,1024]{1,0:T(8,128)(2,1)S(1)}, bf16[64,1024]{1,0:T(8,128)(2,1)S(1)}, u32[]{:S(2)}, u32[]{:S(2)}) collective-permute-start(bf16[64,1024]{1,0:T(8,128)(2,1)S(1)} %get-tuple-element.6.after_ref), channel_id=1, source_target_pairs={{0,16},{16,0},{1,17},{17,1},{2,18},{18,2},{3,19},{19,3},{4,20},{20... | collective-permute-start | bytes 393224 | tf_op jit(solution)/shard_map/ppermute | solution.py:194

commit v6 on v5

--- a/solution.py
+++ b/solution.py
@@ -20,12 +20,20 @@
     return jnp.where(slot >= 0, place * CAP + slot, -1)
 
 
-def open_body(out_ref):
-    out_ref[...] = jnp.zeros(out_ref.shape, out_ref.dtype)
-
-
-def select_body(opened_ref, tokens_ref, expert_ref, slot_ref, out_ref):
-    del opened_ref
+def load_body(tokens_hbm, out_ref, sems):
+    block = tokens_hbm.shape[0] // PIECES
+    copies = []
+    for piece in range(PIECES):
+        rows = pl.ds(piece * block, block)
+        copies.append(
+            pltpu.make_async_copy(tokens_hbm.at[rows], out_ref.at[rows], sems.at[piece])
+        )
+        copies[-1].start()
+    for copy in copies:
+        copy.wait()
+
+
+def select_body(tokens_ref, expert_ref, slot_ref, out_ref):
     slots, count = out_ref.shape[0], tokens_ref.shape[0]
     flat = slot_of(expert_ref[...], slot_ref[...], slots // CAP)
     rows = lax.broadcasted_iota(jnp.int32, (slots, count), 0)
@@ -143,20 +151,22 @@
     expert_row = routes_expert.reshape(1, count)
     slot_row = route_slot.reshape(1, count)
     long = pl.CostEstimate(flops=20 * 10**9, bytes_accessed=32 * MIB, transcendentals=0)
-    opened = pl.pallas_call(
-        open_body,
-        out_shape=jax.ShapeDtypeStruct((8, 128), jnp.float32),
-        compiler_params=params(8),
+    tokens = pl.pallas_call(
+        load_body,
+        in_specs=[anywhere],
+        out_specs=whole,
+        out_shape=jax.ShapeDtypeStruct((count, width), jnp.bfloat16),
+        scratch_shapes=[pltpu.SemaphoreType.DMA((PIECES,))],
+        compiler_params=params(53),
         cost_estimate=long,
-        name="open",
-    )()
+        name="load",
+    )(tokens)
     values = pl.pallas_call(
         select_body,
-        in_specs=[anywhere] + [whole] * 3,
         out_shape=jax.ShapeDtypeStruct((slots, width), jnp.float32),
         compiler_params=params(8),
         name="select",
-    )(opened, tokens, expert_row, slot_row)
+    )(tokens, expert_row, slot_row)
     outgoing = pl.pallas_call(
         norm_body,
         out_shape=jax.ShapeDtypeStruct((experts, CAP, width), jnp.bfloat16),

time: 31.1 us -> 31.2 us (level)
  Pallas kernels: 3.44 us -> 4.6 us
  local copies, waits for them, and re-layouts: 1.02 us -> 0.03 us
    pallas_call x2, Pallas kernels: 0.2 us -> 1.35 us  [the longest x1 1.15 us: per_device(): pl.pallas_call(load_body, in_specs=[anywhere], out_specs=whole, out_shape...]
    unnamed x14 -> x12, local copies, waits for them, and re-layouts: 1.02 us -> 0.03 us
where the time goes in v6:
time: 31.2 us; the launch traced here: 30.7 us
  blocking collectives  22.1 us (71%)
  Pallas kernels  4.6 us (15%)
  waiting for transfers between devices  1.68 us (5%)
  starting transfers between devices  1.55 us (5%)
  between operations  0.74 us (2%)
    all_to_all x2, blocking collectives, exchange(): lax.all_to_all(blocks, ('dp', 'expert'), split_axis=0, concat_axis=0, til...  22.1 us
    pallas_call x1, Pallas kernels, per_device(): pl.pallas_call(expert_body, out_shape=(jax.ShapeDtypeStruct((slots, width...  1.45 us
    pallas_call x1, Pallas kernels, per_device(): pl.pallas_call(combine_body, in_specs=[whole] * 4, out_specs=[anywhere] *...  1.2 us
    pallas_call x1, Pallas kernels, per_device(): pl.pallas_call(load_body, in_specs=[anywhere], out_specs=whole, out_shape...  1.15 us
    ppermute x1, starting transfers between devices, per_device(): other = lax.ppermute(own, 'dp', swap)  1.13 us
    ppermute x1, waiting for transfers between devices, per_device(): other = lax.ppermute(own, 'dp', swap)  0.99 us
    ppermute x1, waiting for transfers between devices, per_device(): lax.ppermute(send, 'dp', swap)  0.7 us
  transfers between devices with their start and end apart: 2, of which 2 were waited for; matrix products, arithmetic and copies ran while one was open for 0% of the time, Pallas kernels for 1%

profile of v6, /device:TPU:0, one launch (start us, length us, event | category | flops | bytes accessed | tf_op | source)
XLA Modules:
  0.0 30.7 jit_solution(18087763237275198817)
XLA Ops:
  0.6 0.0 copy-start.4
  0.6 0.0 copy-start.3
  0.7 0.0 copy-start.5
  0.7 1.1 %load.1.tokens_ref = bf16[256,1024]{1,0:T(8,128)(2,1)S(1)} custom-call(bf16[256,1024]{1,0:T(8,128)(2,1)} %tokens_hbm.1), custom_call_target="tpu_custom_call" | custom-call | flops 20000000000 | bytes 33554432 | tf_op jit(solution)/shard_map/load/pallas_call | solution.py:154
  1.8 0.0 copy-done.4
  1.8 0.0 copy-done.3
  1.8 0.2 select.1.values_ref
  2.0 0.0 copy-done.5
  2.1 0.0 copy-start
  2.1 0.0 copy-start.1
  2.1 0.2 norm.1.normed_ref
  2.3 12.3 %all_to_all.10.own_ref = bf16[16,4,1024]{2,1,0:T(4,128)(2,1)S(1)} all-to-all(bf16[16,4,1024]{2,1,0:T(4,128)(2,1)S(1)} %norm.1.normed_ref), channel_id=1, replica_groups={{26,27,28,29,30,31,0,1,2,3,4,5,6,7,24,25},{10,11,12,13,14,15,16,17,18,1..., dimensions={0} | all-to-all | bytes 262144 | tf_op jit(solution)/shard_map/all_to_all | solution.py:134
  14.6 1.1 %collective-permute-start = (bf16[16,4,1024]{2,1,0:T(4,128)(2,1)S(1)}, bf16[16,4,1024]{2,1,0:T(4,128)(2,1)S(1)}, u32[]{:S(2)}, u32[]{:S(2)}) collective-permute-start(bf16[16,4,1024]{2,1,0:T(4,128)(2,1)S(1)} %all_to_all.10.own_ref), channel_id=1, source_target_pairs={{0,16},{16,0},{1,17},{17,1},{2,18},{18,2},{3,19},{19,3},{4,20},{20... | collective-permute-start | bytes 393224 | tf_op jit(solution)/shard_map/ppermute | solution.py:178
  15.7 1.0 %collective-permute-done.other_ref = bf16[16,4,1024]{2,1,0:T(4,128)(2,1)S(1)} collective-permute-done((bf16[16,4,1024]{2,1,0:T(4,128)(2,1)S(1)}, bf16[16,4,1024]{2,1,0:T(4,128)(2,1)S(1)}, u32[]{:S(2)}, u32[]{:S(2)}) %collective-permute-start) | collective-permute-done | bytes 131104 | tf_op jit(solution)/shard_map/ppermute | solution.py:178
  16.7 0.0 copy-done
  16.7 0.0 copy-done.1
  16.7 0.0 copy-start.2
  16.7 1.5 %experts.1 = (f32[64,1024]{1,0:T(8,128)S(1)}, bf16[64,1024]{1,0:T(8,128)(2,1)S(1)}) custom-call(bf16[16,4,1024]{2,1,0:T(4,128)(2,1)S(1)} %all_to_all.10.own_ref, bf16[16,4,1024]{2,1,0:T(4,128)(2,1)S(1)} %collective-permute-done.other_ref, bf16[1024,2048]{1,0:T(8,128)(2,1)S(1)} %bitcast.6, bf16[2048,1024]{1,0:T(8,128)(2,1)S(1)} %bitcast.7), custom_call_target="tpu_custom_call" | custom-call | tf_op jit(solution)/shard_map/experts/pallas_call | solution.py:179
  18.2 0.4 %collective-permute-start.1 = (bf16[64,1024]{1,0:T(8,128)(2,1)S(1)}, bf16[64,1024]{1,0:T(8,128)(2,1)S(1)}, u32[]{:S(2)}, u32[]{:S(2)}) collective-permute-start(bf16[64,1024]{1,0:T(8,128)(2,1)S(1)} %get-tuple-element.6.after_ref), channel_id=1, source_target_pairs={{0,16},{16,0},{1,17},{17,1},{2,18},{18,2},{3,19},{19,3},{4,20},{20... | collective-permute-start | bytes 393224 | tf_op jit(solution)/shard_map/ppermute | solution.py:204
  18.6 0.0 copy-done.2
  18.6 0.3 gate.1
  18.9 0.7 %collective-permute-done.1.other_ref = bf16[64,1024]{1,0:T(8,128)(2,1)S(1)} collective-permute-done((bf16[64,1024]{1,0:T(8,128)(2,1)S(1)}, bf16[64,1024]{1,0:T(8,128)(2,1)S(1)}, u32[]{:S(2)}, u32[]{:S(2)}) %collective-permute-start.1) | collective-permute-done | bytes 131104 | tf_op jit(solution)/shard_map/ppermute | solution.py:204
  19.6 0.1 join.1
  19.7 9.9 %all_to_all.11.back_ref = bf16[16,4,1024]{2,1,0:T(4,128)(2,1)S(1)} all-to-all(bf16[16,4,1024]{2,1,0:T(4,128)(2,1)S(1)} %join.1), channel_id=1, replica_groups={{26,27,28,29,30,31,0,1,2,3,4,5,6,7,24,25},{10,11,12,13,14,15,16,17,18,1..., dimensions={0} | all-to-all | bytes 262144 | tf_op jit(solution)/shard_map/all_to_all | solution.py:134
  29.5 1.2 %combine.1 = (bf16[256,1024]{1,0:T(8,128)(2,1)}, bf16[256,1024]{1,0:T(8,128)(2,1)}) custom-call(bf16[256,1024]{1,0:T(8,128)(2,1)S(1)} %load.1.tokens_ref, bf16[256,64]{1,0:T(8,128)(2,1)S(1)} %get-tuple-element.7.pick_ref, f32[256,128]{1,0:T(8,128)S(1)} %get-tuple-element.8.after_ref.gate_ref, bf16[16,4,1024]{2,1,0:T(4,128)(2,1)S(1)} %all_to_all.11.back_ref), custom_call_target="tpu_custom_call" | custom-call | tf_op jit(solution)/shard_map/combine/pallas_call | solution.py:206
Async XLA Ops:
  0.6 1.2 %copy-start.4 = (s32[256]{0:T(256)S(1)}, s32[256]{0:T(256)}, u32[]{:S(2)}) copy-start(s32[256]{0:T(256)} %param.11) | copy-start | bytes 3076
  0.6 1.2 %copy-start.3 = (s32[256]{0:T(256)S(1)}, s32[256]{0:T(256)}, u32[]{:S(2)}) copy-start(s32[256]{0:T(256)} %param.10) | copy-start | bytes 3076
  0.7 1.4 %copy-start.5 = (f32[1024]{0:T(1024)S(1)}, f32[1024]{0:T(1024)}, u32[]{:S(2)}) copy-start(f32[1024]{0:T(1024)} %param.8) | copy-start | bytes 12292
  2.1 14.7 %copy-start = (bf16[1,1024,2048]{2,1,0:T(8,128)(2,1)S(1)}, bf16[1,1024,2048]{2,1,0:T(8,128)(2,1)}, u32[]{:S(2)}) copy-start(bf16[1,1024,2048]{2,1,0:T(8,128)(2,1)} %param.12) | copy-start | bytes 12582916
  2.1 14.7 %copy-start.1 = (bf16[1,2048,1024]{2,1,0:T(8,128)(2,1)S(1)}, bf16[1,2048,1024]{2,1,0:T(8,128)(2,1)}, u32[]{:S(2)}) copy-start(bf16[1,2048,1024]{2,1,0:T(8,128)(2,1)} %param.13) | copy-start | bytes 12582916
  14.6 2.1 %collective-permute-start = (bf16[16,4,1024]{2,1,0:T(4,128)(2,1)S(1)}, bf16[16,4,1024]{2,1,0:T(4,128)(2,1)S(1)}, u32[]{:S(2)}, u32[]{:S(2)}) collective-permute-start(bf16[16,4,1024]{2,1,0:T(4,128)(2,1)S(1)} %all_to_all.10.own_ref), channel_id=1, source_target_pairs={{0,16},{16,0},{1,17},{17,1},{2,18},{18,2},{3,19},{19,3},{4,20},{20... | collective-permute-start | bytes 393224 | tf_op jit(solution)/shard_map/ppermute | solution.py:178
  16.7 1.9 %copy-start.2 = (bf16[1024,16]{0,1:T(8,128)(2,1)S(1)}, bf16[1024,16]{0,1:T(8,128)(2,1)}, u32[]{:S(2)}) copy-start(bf16[1024,16]{0,1:T(8,128)(2,1)} %param.9) | copy-start | bytes 98308
  18.2 1.4 %collective-permute-start.1 = (bf16[64,1024]{1,0:T(8,128)(2,1)S(1)}, bf16[64,1024]{1,0:T(8,128)(2,1)S(1)}, u32[]{:S(2)}, u32[]{:S(2)}) collective-permute-start(bf16[64,1024]{1,0:T(8,128)(2,1)S(1)} %get-tuple-element.6.after_ref), channel_id=1, source_target_pairs={{0,16},{16,0},{1,17},{17,1},{2,18},{18,2},{3,19},{19,3},{4,20},{20... | collective-permute-start | bytes 393224 | tf_op jit(solution)/shard_map/ppermute | solution.py:204

commit v7 on v5

--- a/solution.py
+++ b/solution.py
@@ -24,17 +24,14 @@
     out_ref[...] = jnp.zeros(out_ref.shape, out_ref.dtype)
 
 
-def select_body(opened_ref, tokens_ref, expert_ref, slot_ref, out_ref):
+def dispatch_body(opened_ref, tokens_ref, gain_ref, expert_ref, slot_ref, out_ref):
     del opened_ref
-    slots, count = out_ref.shape[0], tokens_ref.shape[0]
-    flat = slot_of(expert_ref[...], slot_ref[...], slots // CAP)
+    experts, cap, width = out_ref.shape
+    slots, count = experts * cap, tokens_ref.shape[0]
+    flat = slot_of(expert_ref[...], slot_ref[...], experts)
     rows = lax.broadcasted_iota(jnp.int32, (slots, count), 0)
     select = jnp.where(rows == flat, 1.0, 0.0).astype(jnp.bfloat16)
-    out_ref[...] = jnp.dot(select, tokens_ref[...], preferred_element_type=jnp.float32)
-
-
-def norm_body(values_ref, gain_ref, out_ref):
-    values = values_ref[...]
+    values = jnp.dot(select, tokens_ref[...], preferred_element_type=jnp.float32)
     mean = jnp.mean(values, axis=1, keepdims=True)
     centred = values - mean
     var = jnp.mean(centred * centred, axis=1, keepdims=True)
@@ -150,20 +147,14 @@
         cost_estimate=long,
         name="open",
     )()
-    values = pl.pallas_call(
-        select_body,
-        in_specs=[anywhere] + [whole] * 3,
-        out_shape=jax.ShapeDtypeStruct((slots, width), jnp.float32),
-        compiler_params=params(8),
-        name="select",
-    )(opened, tokens, expert_row, slot_row)
     outgoing = pl.pallas_call(
-        norm_body,
+        dispatch_body,
+        in_specs=[anywhere] + [whole] * 4,
         out_shape=jax.ShapeDtypeStruct((experts, CAP, width), jnp.bfloat16),
         compiler_params=params(8),
         cost_estimate=long,
-        name="norm",
-    )(values, ln_gain.reshape(1, width))
+        name="dispatch",
+    )(opened, tokens, ln_gain.reshape(1, width), expert_row, slot_row)
     own = exchange(outgoing)
     other = lax.ppermute(own, "dp", swap)
     keep, send = pl.pallas_call(

time: 31.1 us -> 31 us (level)
  no operation moved by 1% of the time
where the time goes in v7:
time: 31 us; the launch traced here: 30.5 us
  blocking collectives  22.1 us (71%)
  Pallas kernels  3.42 us (11%)
  waiting for transfers between devices  1.67 us (5%)
  starting transfers between devices  1.56 us (5%)
  local copies, waits for them, and re-layouts  1.02 us (3%)
  between operations  0.72 us (2%)
    all_to_all x2, blocking collectives, exchange(): lax.all_to_all(blocks, ('dp', 'expert'), split_axis=0, concat_axis=0, til...  22.1 us
    pallas_call x1, Pallas kernels, per_device(): pl.pallas_call(expert_body, out_shape=(jax.ShapeDtypeStruct((slots, width...  1.44 us
    pallas_call x1, Pallas kernels, per_device(): pl.pallas_call(combine_body, in_specs=[whole] * 4, out_specs=[anywhere] *...  1.2 us
    ppermute x1, starting transfers between devices, per_device(): other = lax.ppermute(own, 'dp', swap)  1.13 us
    unnamed x14, local copies, waits for them, and re-layouts  1.02 us
    ppermute x1, waiting for transfers between devices, per_device(): other = lax.ppermute(own, 'dp', swap)  0.99 us
    ppermute x1, waiting for transfers between devices, per_device(): lax.ppermute(send, 'dp', swap)  0.69 us
  transfers between devices with their start and end apart: 2, of which 2 were waited for; matrix products, arithmetic and copies ran while one was open for 0% of the time, Pallas kernels for 1%

profile of v7, /device:TPU:0, one launch (start us, length us, event | category | flops | bytes accessed | tf_op | source)
XLA Modules:
  0.0 30.5 jit_solution(7762966378911188381)
XLA Ops:
  0.6 0.0 copy-start.2
  0.6 0.0 copy-start.5
  0.7 0.0 copy-start.4
  0.7 0.0 copy-start.6
  0.7 1.0 %copy-done.2 = bf16[256,1024]{1,0:T(8,128)(2,1)S(1)} copy-done((bf16[256,1024]{1,0:T(8,128)(2,1)S(1)}, bf16[256,1024]{1,0:T(8,128)(2,1)}, u32[]{:S(2)}) %copy-start.2) | copy-done | bytes 524312
  1.7 0.0 copy-done.5
  1.7 0.0 copy-done.4
  1.7 0.0 copy-done.6
  1.7 0.0 copy-start
  1.7 0.0 copy-start.1
  1.7 0.4 %dispatch.1.normed_ref = bf16[16,4,1024]{2,1,0:T(4,128)(2,1)S(1)} custom-call(f32[8,128]{1,0:T(8,128)S(1)} %open.1.opened_ref, bf16[256,1024]{1,0:T(8,128)(2,1)S(1)} %copy-done.2, f32[1,1024]{1,0:T(1,128)S(1)} %bitcast.13, s32[1,256]{1,0:T(1,128)S(1)} %bitcast.9, s32[1,256]{1,0:T(1,128)S(1)} %bitcast.11), custom_call_target="tpu_custom_call" | custom-call | flops 20000000000 | bytes 33554432 | tf_op jit(solution)/shard_map/dispatch/pallas_call | solution.py:150
  2.1 12.3 %all_to_all.10.own_ref = bf16[16,4,1024]{2,1,0:T(4,128)(2,1)S(1)} all-to-all(bf16[16,4,1024]{2,1,0:T(4,128)(2,1)S(1)} %dispatch.1.normed_ref), channel_id=1, replica_groups={{26,27,28,29,30,31,0,1,2,3,4,5,6,7,24,25},{10,11,12,13,14,15,16,17,18,1..., dimensions={0} | all-to-all | bytes 262144 | tf_op jit(solution)/shard_map/all_to_all | solution.py:123
  14.4 1.1 %collective-permute-start = (bf16[16,4,1024]{2,1,0:T(4,128)(2,1)S(1)}, bf16[16,4,1024]{2,1,0:T(4,128)(2,1)S(1)}, u32[]{:S(2)}, u32[]{:S(2)}) collective-permute-start(bf16[16,4,1024]{2,1,0:T(4,128)(2,1)S(1)} %all_to_all.10.own_ref), channel_id=1, source_target_pairs={{0,16},{16,0},{1,17},{17,1},{2,18},{18,2},{3,19},{19,3},{4,20},{20... | collective-permute-start | bytes 393224 | tf_op jit(solution)/shard_map/ppermute | solution.py:159
  15.5 1.0 %collective-permute-done.other_ref = bf16[16,4,1024]{2,1,0:T(4,128)(2,1)S(1)} collective-permute-done((bf16[16,4,1024]{2,1,0:T(4,128)(2,1)S(1)}, bf16[16,4,1024]{2,1,0:T(4,128)(2,1)S(1)}, u32[]{:S(2)}, u32[]{:S(2)}) %collective-permute-start) | collective-permute-done | bytes 131104 | tf_op jit(solution)/shard_map/ppermute | solution.py:159
  16.5 0.0 copy-done
  16.5 0.0 copy-done.1
  16.5 0.0 copy-start.3
  16.5 1.4 %experts.1 = (f32[64,1024]{1,0:T(8,128)S(1)}, bf16[64,1024]{1,0:T(8,128)(2,1)S(1)}) custom-call(bf16[16,4,1024]{2,1,0:T(4,128)(2,1)S(1)} %all_to_all.10.own_ref, bf16[16,4,1024]{2,1,0:T(4,128)(2,1)S(1)} %collective-permute-done.other_ref, bf16[1024,2048]{1,0:T(8,128)(2,1)S(1)} %bitcast.6, bf16[2048,1024]{1,0:T(8,128)(2,1)S(1)} %bitcast.7), custom_call_target="tpu_custom_call" | custom-call | tf_op jit(solution)/shard_map/experts/pallas_call | solution.py:160
  18.0 0.4 %collective-permute-start.1 = (bf16[64,1024]{1,0:T(8,128)(2,1)S(1)}, bf16[64,1024]{1,0:T(8,128)(2,1)S(1)}, u32[]{:S(2)}, u32[]{:S(2)}) collective-permute-start(bf16[64,1024]{1,0:T(8,128)(2,1)S(1)} %get-tuple-element.6.after_ref), channel_id=1, source_target_pairs={{0,16},{16,0},{1,17},{17,1},{2,18},{18,2},{3,19},{19,3},{4,20},{20... | collective-permute-start | bytes 393224 | tf_op jit(solution)/shard_map/ppermute | solution.py:185
  18.4 0.0 copy-done.3
  18.4 0.3 gate.1
  18.7 0.7 %collective-permute-done.1.other_ref = bf16[64,1024]{1,0:T(8,128)(2,1)S(1)} collective-permute-done((bf16[64,1024]{1,0:T(8,128)(2,1)S(1)}, bf16[64,1024]{1,0:T(8,128)(2,1)S(1)}, u32[]{:S(2)}, u32[]{:S(2)}) %collective-permute-start.1) | collective-permute-done | bytes 131104 | tf_op jit(solution)/shard_map/ppermute | solution.py:185
  19.4 0.1 join.1
  19.5 9.9 %all_to_all.11.back_ref = bf16[16,4,1024]{2,1,0:T(4,128)(2,1)S(1)} all-to-all(bf16[16,4,1024]{2,1,0:T(4,128)(2,1)S(1)} %join.1), channel_id=1, replica_groups={{26,27,28,29,30,31,0,1,2,3,4,5,6,7,24,25},{10,11,12,13,14,15,16,17,18,1..., dimensions={0} | all-to-all | bytes 262144 | tf_op jit(solution)/shard_map/all_to_all | solution.py:123
  29.3 1.2 %combine.1 = (bf16[256,1024]{1,0:T(8,128)(2,1)}, bf16[256,1024]{1,0:T(8,128)(2,1)}) custom-call(bf16[256,1024]{1,0:T(8,128)(2,1)S(1)} %copy-done.2, bf16[256,64]{1,0:T(8,128)(2,1)S(1)} %get-tuple-element.7.pick_ref, f32[256,128]{1,0:T(8,128)S(1)} %get-tuple-element.8.after_ref.gate_ref, bf16[16,4,1024]{2,1,0:T(4,128)(2,1)S(1)} %all_to_all.11.back_ref), custom_call_target="tpu_custom_call" | custom-call | tf_op jit(solution)/shard_map/combine/pallas_call | solution.py:187
  (1 shorter events, 0.0 us)
Async XLA Ops:
  0.6 1.0 %copy-start.2 = (bf16[256,1024]{1,0:T(8,128)(2,1)S(1)}, bf16[256,1024]{1,0:T(8,128)(2,1)}, u32[]{:S(2)}) copy-start(bf16[256,1024]{1,0:T(8,128)(2,1)} %tokens_ref.3) | copy-start | bytes 1572868
  0.6 1.0 %copy-start.5 = (s32[256]{0:T(256)S(1)}, s32[256]{0:T(256)}, u32[]{:S(2)}) copy-start(s32[256]{0:T(256)} %param.11) | copy-start | bytes 3076
  0.7 1.0 %copy-start.4 = (s32[256]{0:T(256)S(1)}, s32[256]{0:T(256)}, u32[]{:S(2)}) copy-start(s32[256]{0:T(256)} %param.10) | copy-start | bytes 3076
  0.7 1.0 %copy-start.6 = (f32[1024]{0:T(1024)S(1)}, f32[1024]{0:T(1024)}, u32[]{:S(2)}) copy-start(f32[1024]{0:T(1024)} %param.8) | copy-start | bytes 12292
  1.7 14.8 %copy-start = (bf16[1,1024,2048]{2,1,0:T(8,128)(2,1)S(1)}, bf16[1,1024,2048]{2,1,0:T(8,128)(2,1)}, u32[]{:S(2)}) copy-start(bf16[1,1024,2048]{2,1,0:T(8,128)(2,1)} %param.12) | copy-start | bytes 12582916
  1.7 14.8 %copy-start.1 = (bf16[1,2048,1024]{2,1,0:T(8,128)(2,1)S(1)}, bf16[1,2048,1024]{2,1,0:T(8,128)(2,1)}, u32[]{:S(2)}) copy-start(bf16[1,2048,1024]{2,1,0:T(8,128)(2,1)} %param.13) | copy-start | bytes 12582916
  14.4 2.1 %collective-permute-start = (bf16[16,4,1024]{2,1,0:T(4,128)(2,1)S(1)}, bf16[16,4,1024]{2,1,0:T(4,128)(2,1)S(1)}, u32[]{:S(2)}, u32[]{:S(2)}) collective-permute-start(bf16[16,4,1024]{2,1,0:T(4,128)(2,1)S(1)} %all_to_all.10.own_ref), channel_id=1, source_target_pairs={{0,16},{16,0},{1,17},{17,1},{2,18},{18,2},{3,19},{19,3},{4,20},{20... | collective-permute-start | bytes 393224 | tf_op jit(solution)/shard_map/ppermute | solution.py:159
  16.5 1.9 %copy-start.3 = (bf16[1024,16]{0,1:T(8,128)(2,1)S(1)}, bf16[1024,16]{0,1:T(8,128)(2,1)}, u32[]{:S(2)}) copy-start(bf16[1024,16]{0,1:T(8,128)(2,1)} %param.9) | copy-start | bytes 98308
  18.0 1.4 %collective-permute-start.1 = (bf16[64,1024]{1,0:T(8,128)(2,1)S(1)}, bf16[64,1024]{1,0:T(8,128)(2,1)S(1)}, u32[]{:S(2)}, u32[]{:S(2)}) collective-permute-start(bf16[64,1024]{1,0:T(8,128)(2,1)S(1)} %get-tuple-element.6.after_ref), channel_id=1, source_target_pairs={{0,16},{16,0},{1,17},{17,1},{2,18},{18,2},{3,19},{19,3},{4,20},{20... | collective-permute-start | bytes 393224 | tf_op jit(solution)/shard_map/ppermute | solution.py:185

commit v8 on v7

--- a/solution.py
+++ b/solution.py
@@ -11,12 +11,12 @@
 PIECES = 4
 
 
-def rotation(count):
-    return (5 * count) // 8
+def member(place, count):
+    return (place * (count // 2 + 1) + (5 * count) // 8 + 1) % count
 
 
 def slot_of(expert, slot, experts):
-    place = (expert + (experts - rotation(experts))) % experts
+    place = (expert + experts - member(0, experts)) * (experts // 2 + 1) % experts
     return jnp.where(slot >= 0, place * CAP + slot, -1)
 
 
@@ -53,7 +53,7 @@
     exps = jnp.exp(logits - top)
     probs = exps / jnp.sum(exps, axis=0, keepdims=True)
     place = lax.broadcasted_iota(jnp.int32, probs.shape, 1) // CAP
-    owner = (place + rotation(experts)) % experts
+    owner = member(place, experts)
     expert = lax.broadcasted_iota(jnp.int32, probs.shape, 0)
     slot_gate = jnp.sum(jnp.where(owner == expert, probs, 0.0), axis=0, keepdims=True)
     flat = slot_of(expert_ref[...], slot_ref[...], experts)
@@ -117,7 +117,7 @@
 
 def exchange(blocks):
     count = blocks.shape[0]
-    order = [(i + rotation(count)) % count for i in range(count)]
+    order = [member(i, count) for i in range(count)]
     near = [i + count * (i >= count // 2) for i in order]
     far = [i + count * (i < count // 2) for i in order]
     return lax.all_to_all(

time: 31 us -> 30.5 us (0.984)
  the two profiles are of different devices: /device:TPU:0 before, /device:TPU:1 now
where the time goes in v8:
time: 30.5 us; the launch traced here: 30.3 us
  blocking collectives  22.7 us (74%)
  Pallas kernels  3.42 us (11%)
  waiting for transfers between devices  2.25 us (7%)
  local copies, waits for them, and re-layouts  1.02 us (3%)
  between operations  0.72 us (2%)
    all_to_all x2, blocking collectives, exchange(): lax.all_to_all(blocks, ('dp', 'expert'), split_axis=0, concat_axis=0, til...  22.7 us
    pallas_call x1, Pallas kernels, per_device(): pl.pallas_call(expert_body, out_shape=(jax.ShapeDtypeStruct((slots, width...  1.45 us
    ppermute x1, waiting for transfers between devices, per_device(): other = lax.ppermute(own, 'dp', swap)  1.35 us
    pallas_call x1, Pallas kernels, per_device(): pl.pallas_call(combine_body, in_specs=[whole] * 4, out_specs=[anywhere] *...  1.2 us
    unnamed x14, local copies, waits for them, and re-layouts  1.02 us
    ppermute x1, waiting for transfers between devices, per_device(): lax.ppermute(send, 'dp', swap)  0.9 us
  transfers between devices with their start and end apart: 2, of which 2 were waited for; matrix products, arithmetic and copies ran while one was open for 0% of the time, Pallas kernels for 1%

profile of v8, /device:TPU:1, one launch (start us, length us, event | category | flops | bytes accessed | tf_op | source)
XLA Modules:
  0.0 30.3 jit_solution(17437159924458088535)
XLA Ops:
  0.6 0.0 copy-start.2
  0.6 0.0 copy-start.5
  0.7 0.0 copy-start.4
  0.7 0.0 copy-start.6
  0.7 1.0 %copy-done.2 = bf16[256,1024]{1,0:T(8,128)(2,1)S(1)} copy-done((bf16[256,1024]{1,0:T(8,128)(2,1)S(1)}, bf16[256,1024]{1,0:T(8,128)(2,1)}, u32[]{:S(2)}) %copy-start.2) | copy-done | bytes 524312
  1.7 0.0 copy-done.5
  1.7 0.0 copy-done.4
  1.7 0.0 copy-done.6
  1.7 0.0 copy-start
  1.7 0.0 copy-start.1
  1.7 0.4 %dispatch.1.normed_ref = bf16[16,4,1024]{2,1,0:T(4,128)(2,1)S(1)} custom-call(f32[8,128]{1,0:T(8,128)S(1)} %open.1.opened_ref, bf16[256,1024]{1,0:T(8,128)(2,1)S(1)} %copy-done.2, f32[1,1024]{1,0:T(1,128)S(1)} %bitcast.13, s32[1,256]{1,0:T(1,128)S(1)} %bitcast.9, s32[1,256]{1,0:T(1,128)S(1)} %bitcast.11), custom_call_target="tpu_custom_call" | custom-call | flops 20000000000 | bytes 33554432 | tf_op jit(solution)/shard_map/dispatch/pallas_call | solution.py:150
  2.1 12.5 %all_to_all.10.own_ref = bf16[16,4,1024]{2,1,0:T(4,128)(2,1)S(1)} all-to-all(bf16[16,4,1024]{2,1,0:T(4,128)(2,1)S(1)} %dispatch.1.normed_ref), channel_id=1, replica_groups={{27,4,29,6,31,24,1,26,3,28,5,30,7,0,25,2},{11,20,13,22,15,8,17,10,19,12..., dimensions={0} | all-to-all | bytes 262144 | tf_op jit(solution)/shard_map/all_to_all | solution.py:123
  14.6 0.0 collective-permute-start
  14.6 1.3 %collective-permute-done.other_ref = bf16[16,4,1024]{2,1,0:T(4,128)(2,1)S(1)} collective-permute-done((bf16[16,4,1024]{2,1,0:T(4,128)(2,1)S(1)}, bf16[16,4,1024]{2,1,0:T(4,128)(2,1)S(1)}, u32[]{:S(2)}, u32[]{:S(2)}) %collective-permute-start) | collective-permute-done | bytes 131104 | tf_op jit(solution)/shard_map/ppermute | solution.py:159
  15.9 0.0 copy-done
  15.9 0.0 copy-done.1
  15.9 0.0 copy-start.3
  15.9 1.4 %experts.1 = (f32[64,1024]{1,0:T(8,128)S(1)}, bf16[64,1024]{1,0:T(8,128)(2,1)S(1)}) custom-call(bf16[16,4,1024]{2,1,0:T(4,128)(2,1)S(1)} %all_to_all.10.own_ref, bf16[16,4,1024]{2,1,0:T(4,128)(2,1)S(1)} %collective-permute-done.other_ref, bf16[1024,2048]{1,0:T(8,128)(2,1)S(1)} %bitcast.6, bf16[2048,1024]{1,0:T(8,128)(2,1)S(1)} %bitcast.7), custom_call_target="tpu_custom_call" | custom-call | tf_op jit(solution)/shard_map/experts/pallas_call | solution.py:160
  17.4 0.2 collective-permute-start.1
  17.6 0.0 copy-done.3
  17.6 0.3 gate.1
  17.9 0.9 %collective-permute-done.1.other_ref = bf16[64,1024]{1,0:T(8,128)(2,1)S(1)} collective-permute-done((bf16[64,1024]{1,0:T(8,128)(2,1)S(1)}, bf16[64,1024]{1,0:T(8,128)(2,1)S(1)}, u32[]{:S(2)}, u32[]{:S(2)}) %collective-permute-start.1) | collective-permute-done | bytes 131104 | tf_op jit(solution)/shard_map/ppermute | solution.py:185
  18.8 0.1 join.1
  18.9 10.2 %all_to_all.11.back_ref = bf16[16,4,1024]{2,1,0:T(4,128)(2,1)S(1)} all-to-all(bf16[16,4,1024]{2,1,0:T(4,128)(2,1)S(1)} %join.1), channel_id=1, replica_groups={{27,4,29,6,31,24,1,26,3,28,5,30,7,0,25,2},{11,20,13,22,15,8,17,10,19,12..., dimensions={0} | all-to-all | bytes 262144 | tf_op jit(solution)/shard_map/all_to_all | solution.py:123
  29.1 1.2 %combine.1 = (bf16[256,1024]{1,0:T(8,128)(2,1)}, bf16[256,1024]{1,0:T(8,128)(2,1)}) custom-call(bf16[256,1024]{1,0:T(8,128)(2,1)S(1)} %copy-done.2, bf16[256,64]{1,0:T(8,128)(2,1)S(1)} %get-tuple-element.7.pick_ref, f32[256,128]{1,0:T(8,128)S(1)} %get-tuple-element.8.after_ref.gate_ref, bf16[16,4,1024]{2,1,0:T(4,128)(2,1)S(1)} %all_to_all.11.back_ref), custom_call_target="tpu_custom_call" | custom-call | tf_op jit(solution)/shard_map/combine/pallas_call | solution.py:187
  (1 shorter events, 0.0 us)
Async XLA Ops:
  0.6 1.0 %copy-start.2 = (bf16[256,1024]{1,0:T(8,128)(2,1)S(1)}, bf16[256,1024]{1,0:T(8,128)(2,1)}, u32[]{:S(2)}) copy-start(bf16[256,1024]{1,0:T(8,128)(2,1)} %tokens_ref.3) | copy-start | bytes 1572868
  0.6 1.0 %copy-start.5 = (s32[256]{0:T(256)S(1)}, s32[256]{0:T(256)}, u32[]{:S(2)}) copy-start(s32[256]{0:T(256)} %param.11) | copy-start | bytes 3076
  0.7 1.0 %copy-start.4 = (s32[256]{0:T(256)S(1)}, s32[256]{0:T(256)}, u32[]{:S(2)}) copy-start(s32[256]{0:T(256)} %param.10) | copy-start | bytes 3076
  0.7 1.0 %copy-start.6 = (f32[1024]{0:T(1024)S(1)}, f32[1024]{0:T(1024)}, u32[]{:S(2)}) copy-start(f32[1024]{0:T(1024)} %param.8) | copy-start | bytes 12292
  1.7 14.3 %copy-start = (bf16[1,1024,2048]{2,1,0:T(8,128)(2,1)S(1)}, bf16[1,1024,2048]{2,1,0:T(8,128)(2,1)}, u32[]{:S(2)}) copy-start(bf16[1,1024,2048]{2,1,0:T(8,128)(2,1)} %param.12) | copy-start | bytes 12582916
  1.7 14.3 %copy-start.1 = (bf16[1,2048,1024]{2,1,0:T(8,128)(2,1)S(1)}, bf16[1,2048,1024]{2,1,0:T(8,128)(2,1)}, u32[]{:S(2)}) copy-start(bf16[1,2048,1024]{2,1,0:T(8,128)(2,1)} %param.13) | copy-start | bytes 12582916
  14.6 1.3 %collective-permute-start = (bf16[16,4,1024]{2,1,0:T(4,128)(2,1)S(1)}, bf16[16,4,1024]{2,1,0:T(4,128)(2,1)S(1)}, u32[]{:S(2)}, u32[]{:S(2)}) collective-permute-start(bf16[16,4,1024]{2,1,0:T(4,128)(2,1)S(1)} %all_to_all.10.own_ref), channel_id=1, source_target_pairs={{0,16},{16,0},{1,17},{17,1},{2,18},{18,2},{3,19},{19,3},{4,20},{20... | collective-permute-start | bytes 393224 | tf_op jit(solution)/shard_map/ppermute | solution.py:159
  15.9 1.7 %copy-start.3 = (bf16[1024,16]{0,1:T(8,128)(2,1)S(1)}, bf16[1024,16]{0,1:T(8,128)(2,1)}, u32[]{:S(2)}) copy-start(bf16[1024,16]{0,1:T(8,128)(2,1)} %param.9) | copy-start | bytes 98308
  17.4 1.4 %collective-permute-start.1 = (bf16[64,1024]{1,0:T(8,128)(2,1)S(1)}, bf16[64,1024]{1,0:T(8,128)(2,1)S(1)}, u32[]{:S(2)}, u32[]{:S(2)}) collective-permute-start(bf16[64,1024]{1,0:T(8,128)(2,1)S(1)} %get-tuple-element.6.after_ref), channel_id=1, source_target_pairs={{0,16},{16,0},{1,17},{17,1},{2,18},{18,2},{3,19},{19,3},{4,20},{20... | collective-permute-start | bytes 393224 | tf_op jit(solution)/shard_map/ppermute | solution.py:185

commit v9 on v8

--- a/solution.py
+++ b/solution.py
@@ -12,11 +12,11 @@
 
 
 def member(place, count):
-    return (place * (count // 2 + 1) + (5 * count) // 8 + 1) % count
+    return place ^ ((11 * count) // 16)
 
 
 def slot_of(expert, slot, experts):
-    place = (expert + experts - member(0, experts)) * (experts // 2 + 1) % experts
+    place = member(expert, experts)
     return jnp.where(slot >= 0, place * CAP + slot, -1)
 
 

time: 30.5 us -> 30.4 us (level)
  the two profiles are of different devices: /device:TPU:1 before, /device:TPU:0 now
where the time goes in v9:
time: 30.4 us; the launch traced here: 30.1 us
  blocking collectives  22.2 us (73%)
  Pallas kernels  3.43 us (11%)
  waiting for transfers between devices  1.68 us (6%)
  starting transfers between devices  1.08 us (4%)
  local copies, waits for them, and re-layouts  1.02 us (3%)
  between operations  0.72 us (2%)
    all_to_all x2, blocking collectives, exchange(): lax.all_to_all(blocks, ('dp', 'expert'), split_axis=0, concat_axis=0, til...  22.2 us
    pallas_call x1, Pallas kernels, per_device(): pl.pallas_call(expert_body, out_shape=(jax.ShapeDtypeStruct((slots, width...  1.45 us
    pallas_call x1, Pallas kernels, per_device(): pl.pallas_call(combine_body, in_specs=[whole] * 4, out_specs=[anywhere] *...  1.2 us
    unnamed x14, local copies, waits for them, and re-layouts  1.02 us
    ppermute x1, waiting for transfers between devices, per_device(): other = lax.ppermute(own, 'dp', swap)  0.99 us
    ppermute x1, waiting for transfers between devices, per_device(): lax.ppermute(send, 'dp', swap)  0.7 us
    ppermute x1, starting transfers between devices, per_device(): other = lax.ppermute(own, 'dp', swap)  0.66 us
  transfers between devices with their start and end apart: 2, of which 2 were waited for; matrix products, arithmetic and copies ran while one was open for 0% of the time, Pallas kernels for 1%

profile of v9, /device:TPU:0, one launch (start us, length us, event | category | flops | bytes accessed | tf_op | source)
XLA Modules:
  0.0 30.1 jit_solution(18009276124814803205)
XLA Ops:
  0.6 0.0 copy-start.2
  0.6 0.0 copy-start.5
  0.7 0.0 copy-start.4
  0.7 0.0 copy-start.6
  0.7 1.0 %copy-done.2 = bf16[256,1024]{1,0:T(8,128)(2,1)S(1)} copy-done((bf16[256,1024]{1,0:T(8,128)(2,1)S(1)}, bf16[256,1024]{1,0:T(8,128)(2,1)}, u32[]{:S(2)}) %copy-start.2) | copy-done | bytes 524312
  1.7 0.0 copy-done.5
  1.7 0.0 copy-done.4
  1.7 0.0 copy-done.6
  1.7 0.0 copy-start
  1.7 0.0 copy-start.1
  1.7 0.4 %dispatch.1.normed_ref = bf16[16,4,1024]{2,1,0:T(4,128)(2,1)S(1)} custom-call(f32[8,128]{1,0:T(8,128)S(1)} %open.1.opened_ref, bf16[256,1024]{1,0:T(8,128)(2,1)S(1)} %copy-done.2, f32[1,1024]{1,0:T(1,128)S(1)} %bitcast.13, s32[1,256]{1,0:T(1,128)S(1)} %bitcast.9, s32[1,256]{1,0:T(1,128)S(1)} %bitcast.11), custom_call_target="tpu_custom_call" | custom-call | flops 20000000000 | bytes 33554432 | tf_op jit(solution)/shard_map/dispatch/pallas_call | solution.py:150
  2.1 11.9 %all_to_all.10.own_ref = bf16[16,4,1024]{2,1,0:T(4,128)(2,1)S(1)} all-to-all(bf16[16,4,1024]{2,1,0:T(4,128)(2,1)S(1)} %dispatch.1.normed_ref), channel_id=1, replica_groups={{27,26,25,24,31,30,29,28,3,2,1,0,7,6,5,4},{11,10,9,8,15,14,13,12,19,18,..., dimensions={0} | all-to-all | bytes 262144 | tf_op jit(solution)/shard_map/all_to_all | solution.py:123
  14.1 0.7 %collective-permute-start = (bf16[16,4,1024]{2,1,0:T(4,128)(2,1)S(1)}, bf16[16,4,1024]{2,1,0:T(4,128)(2,1)S(1)}, u32[]{:S(2)}, u32[]{:S(2)}) collective-permute-start(bf16[16,4,1024]{2,1,0:T(4,128)(2,1)S(1)} %all_to_all.10.own_ref), channel_id=1, source_target_pairs={{0,16},{16,0},{1,17},{17,1},{2,18},{18,2},{3,19},{19,3},{4,20},{20... | collective-permute-start | bytes 393224 | tf_op jit(solution)/shard_map/ppermute | solution.py:159
  14.7 1.0 %collective-permute-done.other_ref = bf16[16,4,1024]{2,1,0:T(4,128)(2,1)S(1)} collective-permute-done((bf16[16,4,1024]{2,1,0:T(4,128)(2,1)S(1)}, bf16[16,4,1024]{2,1,0:T(4,128)(2,1)S(1)}, u32[]{:S(2)}, u32[]{:S(2)}) %collective-permute-start) | collective-permute-done | bytes 131104 | tf_op jit(solution)/shard_map/ppermute | solution.py:159
  15.7 0.0 copy-done
  15.7 0.0 copy-done.1
  15.7 0.0 copy-start.3
  15.7 1.5 %experts.1 = (f32[64,1024]{1,0:T(8,128)S(1)}, bf16[64,1024]{1,0:T(8,128)(2,1)S(1)}) custom-call(bf16[16,4,1024]{2,1,0:T(4,128)(2,1)S(1)} %all_to_all.10.own_ref, bf16[16,4,1024]{2,1,0:T(4,128)(2,1)S(1)} %collective-permute-done.other_ref, bf16[1024,2048]{1,0:T(8,128)(2,1)S(1)} %bitcast.6, bf16[2048,1024]{1,0:T(8,128)(2,1)S(1)} %bitcast.7), custom_call_target="tpu_custom_call" | custom-call | tf_op jit(solution)/shard_map/experts/pallas_call | solution.py:160
  17.2 0.4 %collective-permute-start.1 = (bf16[64,1024]{1,0:T(8,128)(2,1)S(1)}, bf16[64,1024]{1,0:T(8,128)(2,1)S(1)}, u32[]{:S(2)}, u32[]{:S(2)}) collective-permute-start(bf16[64,1024]{1,0:T(8,128)(2,1)S(1)} %get-tuple-element.6.after_ref), channel_id=1, source_target_pairs={{0,16},{16,0},{1,17},{17,1},{2,18},{18,2},{3,19},{19,3},{4,20},{20... | collective-permute-start | bytes 393224 | tf_op jit(solution)/shard_map/ppermute | solution.py:185
  17.6 0.0 copy-done.3
  17.6 0.3 gate.1
  17.9 0.7 %collective-permute-done.1.other_ref = bf16[64,1024]{1,0:T(8,128)(2,1)S(1)} collective-permute-done((bf16[64,1024]{1,0:T(8,128)(2,1)S(1)}, bf16[64,1024]{1,0:T(8,128)(2,1)S(1)}, u32[]{:S(2)}, u32[]{:S(2)}) %collective-permute-start.1) | collective-permute-done | bytes 131104 | tf_op jit(solution)/shard_map/ppermute | solution.py:185
  18.6 0.1 join.1
  18.7 10.3 %all_to_all.11.back_ref = bf16[16,4,1024]{2,1,0:T(4,128)(2,1)S(1)} all-to-all(bf16[16,4,1024]{2,1,0:T(4,128)(2,1)S(1)} %join.1), channel_id=1, replica_groups={{27,26,25,24,31,30,29,28,3,2,1,0,7,6,5,4},{11,10,9,8,15,14,13,12,19,18,..., dimensions={0} | all-to-all | bytes 262144 | tf_op jit(solution)/shard_map/all_to_all | solution.py:123
  28.9 1.2 %combine.1 = (bf16[256,1024]{1,0:T(8,128)(2,1)}, bf16[256,1024]{1,0:T(8,128)(2,1)}) custom-call(bf16[256,1024]{1,0:T(8,128)(2,1)S(1)} %copy-done.2, bf16[256,64]{1,0:T(8,128)(2,1)S(1)} %get-tuple-element.7.pick_ref, f32[256,128]{1,0:T(8,128)S(1)} %get-tuple-element.8.after_ref.gate_ref, bf16[16,4,1024]{2,1,0:T(4,128)(2,1)S(1)} %all_to_all.11.back_ref), custom_call_target="tpu_custom_call" | custom-call | tf_op jit(solution)/shard_map/combine/pallas_call | solution.py:187
  (1 shorter events, 0.0 us)
Async XLA Ops:
  0.6 1.0 %copy-start.2 = (bf16[256,1024]{1,0:T(8,128)(2,1)S(1)}, bf16[256,1024]{1,0:T(8,128)(2,1)}, u32[]{:S(2)}) copy-start(bf16[256,1024]{1,0:T(8,128)(2,1)} %tokens_ref.3) | copy-start | bytes 1572868
  0.6 1.0 %copy-start.5 = (s32[256]{0:T(256)S(1)}, s32[256]{0:T(256)}, u32[]{:S(2)}) copy-start(s32[256]{0:T(256)} %param.11) | copy-start | bytes 3076
  0.7 1.0 %copy-start.4 = (s32[256]{0:T(256)S(1)}, s32[256]{0:T(256)}, u32[]{:S(2)}) copy-start(s32[256]{0:T(256)} %param.10) | copy-start | bytes 3076
  0.7 1.0 %copy-start.6 = (f32[1024]{0:T(1024)S(1)}, f32[1024]{0:T(1024)}, u32[]{:S(2)}) copy-start(f32[1024]{0:T(1024)} %param.8) | copy-start | bytes 12292
  1.7 14.0 %copy-start = (bf16[1,1024,2048]{2,1,0:T(8,128)(2,1)S(1)}, bf16[1,1024,2048]{2,1,0:T(8,128)(2,1)}, u32[]{:S(2)}) copy-start(bf16[1,1024,2048]{2,1,0:T(8,128)(2,1)} %param.12) | copy-start | bytes 12582916
  1.7 14.0 %copy-start.1 = (bf16[1,2048,1024]{2,1,0:T(8,128)(2,1)S(1)}, bf16[1,2048,1024]{2,1,0:T(8,128)(2,1)}, u32[]{:S(2)}) copy-start(bf16[1,2048,1024]{2,1,0:T(8,128)(2,1)} %param.13) | copy-start | bytes 12582916
  14.1 1.6 %collective-permute-start = (bf16[16,4,1024]{2,1,0:T(4,128)(2,1)S(1)}, bf16[16,4,1024]{2,1,0:T(4,128)(2,1)S(1)}, u32[]{:S(2)}, u32[]{:S(2)}) collective-permute-start(bf16[16,4,1024]{2,1,0:T(4,128)(2,1)S(1)} %all_to_all.10.own_ref), channel_id=1, source_target_pairs={{0,16},{16,0},{1,17},{17,1},{2,18},{18,2},{3,19},{19,3},{4,20},{20... | collective-permute-start | bytes 393224 | tf_op jit(solution)/shard_map/ppermute | solution.py:159
  15.7 1.9 %copy-start.3 = (bf16[1024,16]{0,1:T(8,128)(2,1)S(1)}, bf16[1024,16]{0,1:T(8,128)(2,1)}, u32[]{:S(2)}) copy-start(bf16[1024,16]{0,1:T(8,128)(2,1)} %param.9) | copy-start | bytes 98308
  17.2 1.4 %collective-permute-start.1 = (bf16[64,1024]{1,0:T(8,128)(2,1)S(1)}, bf16[64,1024]{1,0:T(8,128)(2,1)S(1)}, u32[]{:S(2)}, u32[]{:S(2)}) collective-permute-start(bf16[64,1024]{1,0:T(8,128)(2,1)S(1)} %get-tuple-element.6.after_ref), channel_id=1, source_target_pairs={{0,16},{16,0},{1,17},{17,1},{2,18},{18,2},{3,19},{19,3},{4,20},{20... | collective-permute-start | bytes 393224 | tf_op jit(solution)/shard_map/ppermute | solution.py:185
